TPU v7x, 256 devices: a whole 4x4x8 slice. The times are simulated.
256 devices in a mesh: band: 16 (over y_lo, z), dom: 16 (over x, y_hi, core).
Axes of the slice: x: 4, y: 4 (y_hi: 2, y_lo: 2; y = y_hi * 2 + y_lo), z: 8, core: 2. Of those that a mesh axis runs over, the one named last changes fastest.
Arguments:
- wavefunctions: float32 [1024, 64, 16, 128], P('band', 'dom'), may hold values from -6 to 6
- potential: float32 [64, 16, 128], P('dom'), may hold values from -40 to 40
- projectors: float32 [64, 18, 4, 16, 128], P('dom'), may hold values from -0.0625 to 0.0625
- hamiltonian_correction: float32 [64, 18, 18], P('dom'), may hold values from -0.0390625 to 0.0390625
- delta_s: float32 [64, 18, 18], P('dom'), may hold values from -0.0390625 to 0.0390625
- projector_count: int32 [64], P('dom'), may hold values from 1 to 18
Outputs:
- ham: float32 [1024, 1024], P('band')
- correlation: float32 [1024, 1024], P('band')
All inputs are finite; a program needn't handle non-finite values.
Results may differ from a plain program's by a relative error of at most 0.00007.
Values sent between devices are 32-bit elements; how exact they have to be, the bound alone decides.
A program may use at most 192 MiB of HBM per device.

v0:
```python
import jax
import jax.numpy as jnp
from jax import lax
from jax.sharding import PartitionSpec as P


def with_halo(cells, sides, width):
    for axis, dim in sides:
        count = lax.axis_size(axis)
        head = lax.slice_in_dim(cells, 0, width, axis=dim)
        tail = lax.slice_in_dim(cells, cells.shape[dim] - width, cells.shape[dim], axis=dim)
        cells = jnp.concatenate(
            [
                lax.ppermute(tail, axis, [(i, (i + 1) % count) for i in range(count)]),
                cells,
                lax.ppermute(head, axis, [((i + 1) % count, i) for i in range(count)]),
            ],
            axis=dim,
        )
    return cells


def side_by_side(arrays, axis, dim, along):
    columns = [a.reshape(*a.shape[:along], -1) for a in arrays]
    both = jnp.concatenate(columns, axis=along)
    result, at, finished = (lax.all_gather(both, axis, axis=dim, tiled=True), 0, [])
    for a, column in zip(arrays, columns):
        piece = result[..., at : at + column.shape[along]]
        finished.append(piece.reshape(*piece.shape[:along], *a.shape[along:]))
        at += column.shape[along]
    return tuple(finished)


def gathered_total(x, axis):
    return lax.all_gather(x, axis).sum(0)


def rows_product(left, right):
    return lax.dot_general(
        left,
        right,
        (((1,), (1,)), ((), ())),
        precision=lax.Precision.HIGHEST,
        preferred_element_type=jnp.float32,
    )


def kinetic_apply(padded, wavefn, potential):
    beside = padded[:, 2:] + padded[:, :-2]
    beside = beside + jnp.roll(wavefn, 1, 2) + jnp.roll(wavefn, -1, 2)
    beside = beside + jnp.roll(wavefn, 1, 3) + jnp.roll(wavefn, -1, 3)
    return 0.5 * (6.0 * wavefn - beside) + potential[None] * wavefn


def coefficients(flat_part, projector_flattened, slot_mask):
    return rows_product(flat_part, projector_flattened) * slot_mask[None, :]


def pair_blocks(own, piece_flat, piece_coef):
    hpsi_flat, psi_flat, coupled_h, coupled_s, volume = own
    ham_block = volume * rows_product(hpsi_flat, piece_flat) + rows_product(coupled_h, piece_coef)
    ovl_block = volume * rows_product(psi_flat, piece_flat) + rows_product(coupled_s, piece_coef)
    return (ham_block, ovl_block)


def place_blocks(blocks):
    ham_rows = blocks[0]
    ovl_rows = blocks[1]
    return (ham_rows, ovl_rows)


def on_device(
    wavefunctions, potential, projectors, hamiltonian_correction, delta_s, projector_count
):
    band_count, cx, ny, nz = wavefunctions.shape
    grid_cells = cx * ny * nz
    volume = 1.0 / (grid_cells * lax.axis_size("dom"))
    padded = with_halo(wavefunctions, (("dom", 1),), 1)
    hpsi = kinetic_apply(padded, wavefunctions, potential)
    psi_flat = wavefunctions.reshape(band_count, grid_cells)
    hpsi_flat = hpsi.reshape(band_count, grid_cells)
    atom_list = hamiltonian_correction.shape[0]
    slot_count = hamiltonian_correction.shape[1]
    slot_mask = (
        (jnp.arange(slot_count, dtype=jnp.int32)[None, :] < projector_count[:, None])
        .astype(jnp.float32)
        .reshape(-1)
    )
    projector_flattened = projectors.reshape(atom_list * slot_count, grid_cells)
    projector_coefficient = coefficients(psi_flat, projector_flattened, slot_mask)
    sym_h = 0.5 * (hamiltonian_correction + jnp.swapaxes(hamiltonian_correction, 1, 2))
    sym_s = 0.5 * (delta_s + jnp.swapaxes(delta_s, 1, 2))
    coefficient_triple = projector_coefficient.reshape(band_count, atom_list, slot_count)
    coupled_h = jnp.einsum(
        "bap,apq->baq", coefficient_triple, sym_h, precision=lax.Precision.HIGHEST
    ).reshape(band_count, -1)
    coupled_s = jnp.einsum(
        "bap,apq->baq", coefficient_triple, sym_s, precision=lax.Precision.HIGHEST
    ).reshape(band_count, -1)
    own = (hpsi_flat, psi_flat, coupled_h, coupled_s, volume)
    piece = side_by_side((wavefunctions, projector_coefficient), "band", 0, 1)
    rows = piece[0].shape[0]
    blocks = pair_blocks(own, piece[0].reshape(rows, grid_cells), piece[1])
    summed = place_blocks(blocks)
    reduced = (gathered_total(summed[0], "dom"), gathered_total(summed[1], "dom"))
    ham = reduced[0]
    correlation = reduced[1]
    return (ham, correlation)


def solution(mesh):
    placed = (
        P("band", "dom", None, None),
        P("dom", None, None),
        P("dom", None, None, None, None),
        P("dom", None, None),
        P("dom", None, None),
        P("dom"),
    )
    return jax.shard_map(
        on_device,
        mesh=mesh,
        in_specs=placed,
        out_specs=(P("band", None), P("band", None)),
        check_vma=False,
    )
```

profile of v0, /device:TPU:1, one launch (start us, length us, event | category | flops | bytes accessed | tf_op | source)
XLA Modules:
  0.0 554.7 jit_solution(8126949004628108999)
XLA Ops:
  7.2 3.5 reshape.44
  10.7 0.1 fusion.37
  10.8 0.1 reshape.48
  10.9 1.2 copy.36
  12.1 0.5 copy-done.1
  12.6 3.1 convolution_multiply_fusion
  15.7 1.5 pad_maximum_fusion
  17.2 1.1 fusion.42
  18.3 3.2 collective-permute-start
  21.5 1.1 collective-permute-start.1
  22.6 0.1 copy.15
  22.7 0.1 copy.14
  22.9 0.3 convolution_bitcast_fusion.1
  23.2 0.8 fusion.38
  24.0 0.8 fusion.39
  24.8 0.2 fusion.41
  25.0 0.5 fusion.40
  25.6 4.1 collective-permute-done
  29.7 5.0 collective-permute-done.1
  34.7 3.3 fusion.13
  38.0 342.0 %all-gather.6.cloned.1.call-done = f32[1024,8264]{1,0:T(8,128)} async-done(((f32[64,8264]{1,0:T(8,128)}), f32[1024,8264]{1,0:T(8,128)}) %all-gather.6.cloned.1.call-update) | async-done | bytes 33849360 | tf_op jit(solution)/shard_map/all_gather | solution.py:26
  380.0 1.8 fusion.31
  381.7 35.7 %fusion.19 = f32[64,1024]{1,0:T(8,128)} fusion(f32[64,1024]{1,0:T(8,128)S(1)} %fusion.31, f32[1024,8264]{1,0:T(8,128)} %all-gather.6.cloned.1.call-done, f32[8,8,64,128]{3,2,1,0:T(8,128)} %bitcast.48), kind=kOutput, calls=%fused_computation.20 | convolution fusion | flops 6442582016 | bytes 36175872 | tf_op jit(solution)/shard_map/dot_general | solution.py:39
  417.5 0.3 all-gather.10.cloned.1.call-start
  417.8 0.1 copy.17
  417.9 0.3 convolution_bitcast_fusion
  418.2 35.0 %fusion.27 = f32[64,1024]{1,0:T(8,128)S(1)} fusion(f32[1024,8264]{1,0:T(8,128)} %all-gather.6.cloned.1.call-done, f32[8,8,64,128]{3,2,1,0:T(8,128)S(1)} %bitcast.47), kind=kOutput, calls=%fused_computation.22 | convolution fusion | flops 6442516480 | bytes 35913728 | tf_op jit(solution)/shard_map/dot_general | solution.py:39
  453.2 2.5 convolution_add_fusion
  455.7 26.5 %all-gather.8.cloned.1.call-done = f32[1024,1024]{1,0:T(8,128)} async-done(((f32[64,1024]{1,0:T(8,128)}), f32[1024,1024]{1,0:T(8,128)}) %all-gather.8.cloned.1.call-update) | async-done | bytes 4194320 | tf_op jit(solution)/shard_map/all_gather | solution.py:35
  482.2 3.2 reduce_sum.18
  485.4 59.6 %all-gather.10.cloned.1.call-done = f32[1024,1024]{1,0:T(8,128)} async-done(((f32[64,1024]{1,0:T(8,128)}), f32[1024,1024]{1,0:T(8,128)}) %all-gather.10.cloned.1.call-update) | async-done | bytes 4194320 | tf_op jit(solution)/shard_map/all_gather | solution.py:35
  545.0 3.2 reduce_sum.19
  (21 shorter events, 0.2 us)
Async XLA Ops:
  7.2 3.6 copy-start.5
  7.2 3.7 copy-start
  7.2 372.8 %all-gather.6.cloned.1.call-start = ((), (), s32[]{:S(2)}) async-start(), calls=%async_computation | async-start | bytes 36208640 | tf_op jit(solution)/shard_map/all_gather | solution.py:26
  10.9 1.7 copy-start.1
  17.2 5.6 %copy-start.2 = (f32[4,18,18]{2,0,1:T(4,128)S(1)}, f32[4,18,18]{2,0,1:T(4,128)}, u32[]{:S(2)}) copy-start(f32[4,18,18]{2,0,1:T(4,128)} %param.9) | copy-start | bytes 15556
  17.2 465.0 %all-gather.8.cloned.1.call-start = ((), (), s32[]{:S(2)}) async-start(), calls=%async_computation.1 | async-start | bytes 4456448 | tf_op jit(solution)/shard_map/all_gather | solution.py:35
  18.3 11.4 %collective-permute-start = (f32[64,1,16,128]{3,2,1,0:T(8,128)}, f32[64,1,16,128]{3,2,1,0:T(8,128)S(1)}, u32[]{:S(2)}, u32[]{:S(2)}) collective-permute-start(f32[64,1,16,128]{3,2,1,0:T(8,128)} %get-tuple-element.10), channel_id=1, source_target_pairs={{1,0},{2,1},{3,2},{4,3},{5,4},{6,5},{7,6},{8,7},{9,8},{10,9},{11,1... | collective-permute-start | bytes 1572872 | tf_op jit(solution)/shard_map/ppermute | solution.py:16
  21.5 13.2 %collective-permute-start.1 = (f32[64,1,16,128]{3,2,1,0:T(8,128)}, f32[64,1,16,128]{3,2,1,0:T(8,128)S(1)}, u32[]{:S(2)}, u32[]{:S(2)}) collective-permute-start(f32[64,1,16,128]{3,2,1,0:T(8,128)} %get-tuple-element.11), channel_id=1, source_target_pairs={{0,1},{1,2},{2,3},{3,4},{4,5},{5,6},{6,7},{7,8},{8,9},{9,10},{10,1... | collective-permute-start | bytes 1572872 | tf_op jit(solution)/shard_map/ppermute | solution.py:14
  25.0 9.7 %copy-start.4 = (f32[4,16,128]{2,1,0:T(8,128)S(1)}, f32[4,16,128]{2,1,0:T(8,128)}, u32[]{:S(2)}) copy-start(f32[4,16,128]{2,1,0:T(8,128)} %param.7) | copy-start | bytes 98308
  381.7 36.0 %copy-start.3 = (f32[4,18,18]{2,0,1:T(4,128)S(1)}, f32[4,18,18]{2,0,1:T(4,128)}, u32[]{:S(2)}) copy-start(f32[4,18,18]{2,0,1:T(4,128)} %param.10) | copy-start | bytes 15556
  417.5 127.6 %all-gather.10.cloned.1.call-start = ((), (), s32[]{:S(2)}) async-start(), calls=%async_computation.2 | async-start | bytes 4456448 | tf_op jit(solution)/shard_map/all_gather | solution.py:35
Sparse Core Ops, SparseCore 0:
  17.3 362.6 all-gather.5
  417.6 64.5 all-gather.7
  484.9 60.0 all-gather.9
where the time goes:
time: 555 us
  waiting for transfers between devices  437 us (79%)
  matrix products  78.7 us (14%)
  between operations  13.9 us (3%)
  other arithmetic  11.3 us (2%)
  local copies, waits for them, and re-layouts  9.05 us (2%)
    all_gather x1, waiting for transfers between devices, side_by_side(): lax.all_gather(both, axis, axis=dim, tiled=True)  342 us
    all_gather x2, waiting for transfers between devices, gathered_total(): return lax.all_gather(x, axis).sum(0)  86.1 us
    dot_general x5, matrix products, rows_product(): lax.dot_general(left, right, (((1,), (1,)), ((), ())), precision=lax.Prec...  78.1 us
  transfers between devices with their start and end apart: 5, of which 5 were waited for; matrix products, arithmetic and copies ran while one was open for 9% of the time, Pallas kernels for 0%

commit v1 on v0

v1 whole, which is shorter than its diff:
```python
import functools

import jax
import jax.numpy as jnp
from jax import lax
from jax.experimental import pallas as pl
from jax.experimental.pallas import tpu as pltpu
from jax.sharding import PartitionSpec as P

MESH = pl.DeviceIdType.MESH
F32 = jnp.float32
BF16 = jnp.bfloat16
NB = 16
ND = 16
CH = 8
RPZ = 32
CHUNK = (CH + 1) * RPZ
VOLUME = 1.0 / 131072.0
OFFSETS = [(0, 1), (0, -1), (1, 1), (1, -1), (0, 2), (0, -2), (1, 2), (1, -2), (1, 0),
           (0, 3), (0, -3), (1, 3), (1, -3), (0, 4), (1, 4)]


def split(x):
    hi = x.astype(BF16)
    return hi, (x - hi.astype(F32)).astype(BF16)


def dot(a, b):
    return lax.dot_general(a, b, (((1,), (0,)), ((), ())), preferred_element_type=F32)


def dot_nt(a, b):
    return lax.dot_general(a, b, (((1,), (1,)), ((), ())), preferred_element_type=F32)


def kernel(psi, pot, proj, ext, out, T, R, RX, CS, CR, VB, AF, AThi, ATlo, Bhi, Blo, ATC, BC,
           ssem, rsem, cssem, crsem, xssem, xrsem):
    g = lax.axis_index("band")
    d = lax.axis_index("dom")
    ylo, z = g // 8, lax.rem(g, 8)
    dprev, dnext = lax.rem(d + ND - 1, ND), lax.rem(d + 1, ND)

    def peer(o):
        dy, dz = OFFSETS[o]
        return lax.rem(ylo + dy, 2) * 8 + lax.rem(z + dz + 8, 8)

    def source(o):
        dy, dz = OFFSETS[o]
        return lax.rem(ylo + dy, 2) * 8 + lax.rem(z - dz + 8, 8)

    barrier = pltpu.get_barrier_semaphore()
    for o in range(NB - 1):
        pl.semaphore_signal(barrier, inc=1, device_id={"band": peer(o)}, device_id_type=MESH)
    pl.semaphore_signal(barrier, inc=1, device_id={"dom": dprev}, device_id_type=MESH)
    pl.semaphore_signal(barrier, inc=1, device_id={"dom": dnext}, device_id_type=MESH)

    for r in range(RPZ):
        xy = (r // 8) * 16 + r % 8
        a = psi[pl.ds(xy, 64, stride=64), :]
        b = psi[pl.ds(xy + 8, 64, stride=64), :]
        T[pl.ds(r, 128, stride=RPZ), :] = jnp.concatenate([a, b], axis=0).T
    T[pl.ds(128 * RPZ, RPZ), :] = T[pl.ds(0, RPZ), :]

    pl.semaphore_wait(barrier, NB + 1)

    def main_copy(o):
        p = peer(o)
        return pltpu.make_async_remote_copy(
            src_ref=T.at[pl.ds(pl.multiple_of(p * (CH * RPZ), CH * RPZ), CHUNK)],
            dst_ref=R.at[g],
            send_sem=ssem.at[o], recv_sem=rsem.at[o],
            device_id={"band": p}, device_id_type=MESH)

    def coef_copy(o):
        p = peer(o)
        return pltpu.make_async_remote_copy(
            src_ref=CS.at[p], dst_ref=CR.at[g],
            send_sem=cssem.at[o], recv_sem=crsem.at[o],
            device_id={"band": p}, device_id_type=MESH)

    def x_copy(o):
        s = source(o) if o < NB - 1 else g
        return pltpu.make_async_remote_copy(
            src_ref=R.at[s].reshape(CH + 1, RPZ, 128).at[pl.ds(0, CH), pl.ds(0, 8)],
            dst_ref=RX.at[s],
            send_sem=xssem.at[o], recv_sem=xrsem.at[o],
            device_id={"dom": dprev}, device_id_type=MESH)

    for o in range(NB - 1):
        main_copy(o).start()

    R[g] = T[pl.ds(pl.multiple_of(g * (CH * RPZ), CH * RPZ), CHUNK), :]

    acc = jnp.zeros((72, 64), F32)
    for r in range(RPZ):
        xy = (r // 8) * 16 + r % 8
        p = jnp.concatenate([psi[pl.ds(xy, 64, stride=64), :], psi[pl.ds(xy + 8, 64, stride=64), :]], axis=1)
        q = jnp.concatenate([proj[pl.ds(xy, 72, stride=64), :], proj[pl.ds(xy + 8, 72, stride=64), :]], axis=1)
        phi, plo = split(p)
        qhi, qlo = split(q)
        acc = acc + dot_nt(qhi, phi) + dot_nt(qhi, plo) + dot_nt(qlo, phi)
    c = jnp.concatenate([acc, jnp.zeros((56, 64), F32)], axis=0)
    chi, clo = split(c)
    ehi, elo = split(ext[...])
    msg = dot(ehi, chi) + dot(ehi, clo) + dot(elo, chi)
    msg = jnp.concatenate([msg, msg], axis=1)
    CS[...] = msg.reshape(NB, 16, 128)
    CR[g] = CS[g]
    for o in range(NB - 1):
        coef_copy(o).start()

    v = 3.0 + pltpu.roll(pot[...], lax.rem(128 - g * CH, 128), 1)
    for zi in range(CH):
        wide = jnp.broadcast_to(v[:, zi:zi + 1], (64, 128))
        for half in range(2):
            for x in range(4):
                VB[zi, half, x * 8:(x + 1) * 8, :] = wide[x * 16 + half * 8:x * 16 + half * 8 + 8]

    x_copy(NB - 1).start()
    for o in range(NB - 1):
        main_copy(o).wait_recv()
        x_copy(o).start()
    for o in range(NB - 1):
        coef_copy(o).wait_recv()
    for o in range(NB):
        x_copy(o).wait_recv()

    low = lax.broadcasted_iota(jnp.int32, (RPZ, 128), 1) < 64
    low8 = lax.broadcasted_iota(jnp.int32, (8, 128), 1) < 64
    low16 = lax.broadcasted_iota(jnp.int32, (16, 128), 1) < 64
    last = lax.broadcasted_iota(jnp.int32, (8, 128), 0) == 7

    def merge(a, b, mask):
        return jnp.where(mask, a, pltpu.roll(b, 64, 1)), jnp.where(mask, pltpu.roll(a, 64, 1), b)

    def assemble(m, _):
        cols = pl.ds(pl.multiple_of(m * 128, 128), 128)
        cols2 = pl.ds(pl.multiple_of(1024 + m * 128, 128), 128)

        def column(zi):
            rows = pl.ds(pl.multiple_of(zi * RPZ, RPZ), RPZ)
            return merge(R[2 * m, rows, :], R[2 * m + 1, rows, :], low)

        now = column(0)
        for zi in range(CH):
            nxt = column(zi + 1)
            halo = merge(RX[2 * m, zi], RX[2 * m + 1, zi], low8)
            turned = []
            for half in range(2):
                turned.append([pltpu.roll(now[half][x * 8:(x + 1) * 8], 7, 0) for x in range(4)])
            for half in range(2):
                a = now[half]
                ax = jnp.concatenate([a[8:], halo[half]], axis=0)
                ay = jnp.concatenate(
                    [jnp.where(last, turned[1 - half][x], turned[half][x]) for x in range(4)], axis=0)
                h = VB[zi, half] * a - ax - ay - nxt[half]
                rows = pl.ds(half * 256 + zi * RPZ, RPZ)
                AF[rows, :] = a
                hi, lo = split(h)
                Bhi[rows, cols] = hi
                Blo[rows, cols] = lo
                hi, lo = split(a)
                Bhi[rows, cols2] = hi
                Blo[rows, cols2] = lo
            now = nxt
        hi, lo = split(AF[...].T)
        AThi[cols, :] = hi
        ATlo[cols, :] = lo
        cc, _ = merge(CR[2 * m], CR[2 * m + 1], low16)
        chi, clo = split(cc)
        c5 = chi.astype(F32)
        zero = jnp.zeros((16, 128), F32)
        row16 = lax.broadcasted_iota(jnp.int32, (16, 128), 0)
        keep = row16 < 5
        ahi = jnp.where(keep, chi.astype(F32), zero)
        alo = jnp.where(keep, clo.astype(F32), zero)
        stack = jnp.concatenate([ahi, ahi, alo, jnp.zeros((80, 128), F32)], axis=0)
        ATC[cols, :] = stack.T.astype(BF16)
        for t, at in ((1, cols), (2, cols2)):
            bhi = jnp.where(keep, pltpu.roll(chi.astype(F32), 16 - 5 * t, 0), zero)
            blo = jnp.where(keep, pltpu.roll(clo.astype(F32), 16 - 5 * t, 0), zero)
            BC[:, at] = jnp.concatenate([bhi, blo, bhi, jnp.zeros((80, 128), F32)], axis=0).astype(BF16)
        return 0

    lax.fori_loop(0, 8, assemble, 0)

    def product(t, _):
        i, j = t // 8, lax.rem(t, 8)
        rows = pl.ds(pl.multiple_of(i * 256, 256), 256)
        cols = pl.ds(pl.multiple_of(j * 256, 256), 256)
        a = AThi[rows, :]
        res = dot(a, Bhi[:, cols]) + dot(a, Blo[:, cols]) + dot(ATlo[rows, :], Bhi[:, cols]) \
            + dot(ATC[rows, :], BC[:, cols])
        res = res * VOLUME
        out[2 * j, rows, :] = res[:, :128]
        out[2 * j + 1, rows, :] = res[:, 128:]
        return 0

    lax.fori_loop(0, 32, product, 0)

    def symmetrize(t, _):
        i, j = t // 8, lax.rem(t, 8)
        ri = pl.ds(pl.multiple_of(i * 128, 128), 128)
        rj = pl.ds(pl.multiple_of(j * 128, 128), 128)

        @pl.when(i <= j)
        def _():
            s = 0.5 * (out[j, ri, :] + out[i, rj, :].T)
            out[j, ri, :] = s
            out[i, rj, :] = s.T
        return 0

    lax.fori_loop(0, 64, symmetrize, 0)

    for o in range(NB - 1):
        main_copy(o).wait_send()
        coef_copy(o).wait_send()
    for o in range(NB):
        x_copy(o).wait_send()


def couple_matrix(hamiltonian_correction, delta_s, projector_count):
    slot = jnp.arange(18, dtype=jnp.int32)
    mask = (slot[None, :] < projector_count[:, None]).astype(F32)
    both = jnp.stack([hamiltonian_correction, delta_s])
    sym = (0.5 / VOLUME) * (both + jnp.swapaxes(both, 2, 3)) * mask[None, :, :, None] * mask[None, :, None, :]
    eye4 = jnp.eye(4, dtype=F32)
    block = (sym[:, :, :, None, :] * eye4[None, :, None, :, None]).reshape(2, 72, 72)
    block = jnp.concatenate([jnp.eye(72, dtype=F32)[None], block])
    block = jnp.pad(block, ((0, 0), (0, 8), (0, 56))).reshape(3, 16, 5, 128)
    rows = jnp.swapaxes(block, 0, 1).reshape(16, 15, 128)
    return jnp.pad(rows, ((0, 0), (0, 1), (0, 0))).reshape(256, 128)


def on_device(wavefunctions, potential, projectors, hamiltonian_correction, delta_s, projector_count):
    psi = wavefunctions.reshape(4096, 128)
    pot = potential.reshape(64, 128)
    proj = projectors.reshape(72 * 64, 128)
    ext = couple_matrix(hamiltonian_correction, delta_s, projector_count)
    vm = pl.BlockSpec(memory_space=pltpu.VMEM)
    part = pl.pallas_call(
        kernel,
        out_shape=jax.ShapeDtypeStruct((16, 1024, 128), F32),
        in_specs=[vm] * 4,
        out_specs=vm,
        scratch_shapes=[
            pltpu.VMEM((129 * RPZ, 128), F32),
            pltpu.VMEM((NB, CHUNK, 128), F32),
            pltpu.VMEM((NB, CH, 8, 128), F32),
            pltpu.VMEM((NB, 16, 128), F32),
            pltpu.VMEM((NB, 16, 128), F32),
            pltpu.VMEM((CH, 2, RPZ, 128), F32),
            pltpu.VMEM((512, 128), F32),
            pltpu.VMEM((1024, 512), BF16),
            pltpu.VMEM((1024, 512), BF16),
            pltpu.VMEM((512, 2048), BF16),
            pltpu.VMEM((512, 2048), BF16),
            pltpu.VMEM((1024, 128), BF16),
            pltpu.VMEM((128, 2048), BF16),
            pltpu.SemaphoreType.DMA((NB,)),
            pltpu.SemaphoreType.DMA((NB,)),
            pltpu.SemaphoreType.DMA((NB,)),
            pltpu.SemaphoreType.DMA((NB,)),
            pltpu.SemaphoreType.DMA((NB,)),
            pltpu.SemaphoreType.DMA((NB,)),
        ],
        compiler_params=pltpu.CompilerParams(
            collective_id=0, has_side_effects=True, vmem_limit_bytes=60 * 1024 * 1024),
    )(psi, pot, proj, ext)
    rows = lax.psum_scatter(part, "band", scatter_dimension=1, tiled=True)
    total = lax.psum(rows, "dom")
    total = jnp.swapaxes(total.reshape(2, 8, 64, 128), 1, 2).reshape(2, 64, 1024)
    return total[0], total[1]


def solution(mesh):
    placed = (
        P("band", "dom", None, None),
        P("dom", None, None),
        P("dom", None, None, None, None),
        P("dom", None, None),
        P("dom", None, None),
        P("dom"),
    )
    return jax.shard_map(
        on_device, mesh=mesh, in_specs=placed,
        out_specs=(P("band", None), P("band", None)), check_vma=False)
```

time: 555 us -> 363 us (0.65)
  waiting for transfers between devices: 437 us -> 244 us
  Pallas kernels: 0 us -> 98.6 us
  matrix products: 78.7 us -> 0 us
  other arithmetic: 11.3 us -> 3.18 us
    all_gather x3 -> x0, waiting for transfers between devices: 428 us -> none  [the longest x1 342 us: side_by_side(): lax.all_gather(both, axis, axis=dim, tiled=True)]
    psum x0 -> x1, waiting for transfers between devices: none -> 145 us  [on_device(): total = lax.psum(rows, 'dom')]
    pallas_call x0 -> x1, Pallas kernels: none -> 98.6 us  [on_device(): pl.pallas_call(kernel, out_shape=jax.ShapeDtypeStruct((16, 1024, 128), F3...]
    reduce_scatter x0 -> x1, waiting for transfers between devices: none -> 98.4 us  [on_device(): rows = lax.psum_scatter(part, 'band', scatter_dimension=1, tiled=True)]
    dot_general x7 -> x0, matrix products: 78.7 us -> none  [the longest x5 78.1 us: rows_product(): lax.dot_general(left, right, (((1,), (1,)), ((), ())), precision=lax.Prec...]
    ppermute x2 -> x0, waiting for transfers between devices: 9.12 us -> none  [the longest x1 4.99 us: with_halo(): lax.ppermute(tail, axis, [(i, (i + 1) % count) for i in range(count)])]
    reduce_sum x2 -> x0, other arithmetic: 6.37 us -> none  [gathered_total(): return lax.all_gather(x, axis).sum(0)]
  transfers between devices with their start and end apart: 5 -> 2, of which waited for: 5 -> 2; matrix products, arithmetic and copies ran while one was open for 9% -> 0% of each run, Pallas kernels for 0% -> 0%
where the time goes in v1:
time: 363 us
  waiting for transfers between devices  244 us (67%)
  Pallas kernels  98.6 us (27%)
  between operations  14.1 us (4%)
  local copies, waits for them, and re-layouts  3.7 us (1%)
    psum x1, waiting for transfers between devices, on_device(): total = lax.psum(rows, 'dom')  145 us
    pallas_call x1, Pallas kernels, on_device(): pl.pallas_call(kernel, out_shape=jax.ShapeDtypeStruct((16, 1024, 128), F3...  98.6 us
    reduce_scatter x1, waiting for transfers between devices, on_device(): rows = lax.psum_scatter(part, 'band', scatter_dimension=1, tiled=True)  98.4 us
  transfers between devices with their start and end apart: 2, of which 2 were waited for; matrix products, arithmetic and copies ran while one was open for 0% of the time, Pallas kernels for 0%

profile of v1, /device:TPU:1, one launch (start us, length us, event | category | flops | bytes accessed | tf_op | source)
XLA Modules:
  0.0 363.2 jit_solution(2317733786898892974)
XLA Ops:
  7.2 0.0 reduce-scatter.2.cloned.1.call-start
  7.2 0.7 fusion.3
  7.9 0.7 fusion.4
  8.7 0.1 copy.14
  8.8 0.8 pad_maximum_fusion
  9.6 0.1 copy.13
  9.7 0.9 fusion.1
  10.6 0.1 mul.50
  10.7 0.1 mul.51
  10.8 0.1 mul.48
  10.9 0.2 mul.49
  11.2 0.7 pad.9.clone
  11.9 98.6 %shard_map.77 = f32[16,1024,128]{2,1,0:T(8,128)} custom-call(f32[4096,128]{1,0:T(8,128)} %bitcast.26, f32[64,128]{1,0:T(8,128)} %bitcast.37, f32[4608,128]{1,0:T(8,128)} %bitcast.25, f32[256,128]{1,0:T(8,128)} %bitcast.30), custom_call_target="tpu_custom_call" | custom-call | tf_op jit(solution)/shard_map/pallas_call | solution.py:241
  110.5 0.0 reduce-scatter.2.cloned.1.call-update
  110.5 0.0 all-reduce.4.cloned.1.call-start
  110.5 98.4 %reduce-scatter.2.cloned.1.call-done = f32[16,64,128]{2,1,0:T(8,128)} async-done(((f32[16,1024,128]{2,1,0:T(8,128)}), f32[16,64,128]{2,1,0:T(8,128)}) %reduce-scatter.2.cloned.1.call-update) | async-done | bytes 524304 | tf_op jit(solution)/shard_map/reduce_scatter | solution.py:270
  208.9 0.0 all-reduce.4.cloned.1.call-update
  208.9 145.1 %all-reduce.4.cloned.1.call-done = f32[2,64,8,128]{3,1,2,0:T(8,128)} async-done(((f32[2,64,8,128]{3,1,2,0:T(8,128)}), f32[2,64,8,128]{3,1,2,0:T(8,128)}) %all-reduce.4.cloned.1.call-update) | async-done | bytes 524304 | tf_op jit(solution)/shard_map/psum | solution.py:271
  354.1 1.1 fusion.6
  355.1 0.2 copy.19
  355.3 0.2 copy.18
  355.5 0.9 copy_bitcast_fusion
  (8 shorter events, 0.1 us)
Async XLA Ops:
  7.2 201.7 %reduce-scatter.2.cloned.1.call-start = ((), (), s32[]{:S(2)}) async-start(), calls=%async_computation.1 | async-start | bytes 8912896 | tf_op jit(solution)/shard_map/reduce_scatter | solution.py:270
  110.5 243.6 %all-reduce.4.cloned.1.call-start = ((), (), s32[]{:S(2)}) async-start(), calls=%async_computation.2 | async-start | bytes 1048576 | tf_op jit(solution)/shard_map/psum | solution.py:271
Sparse Core Ops, SparseCore 0:
  110.6 98.2 reduce-scatter.1
  211.5 142.5 all-reduce.3

commit v2 on v1

--- a/solution.py
+++ b/solution.py
@@ -33,11 +33,15 @@
     return lax.dot_general(a, b, (((1,), (1,)), ((), ())), preferred_element_type=F32)
 
 
-def kernel(psi, pot, proj, ext, out, T, R, RX, CS, CR, VB, AF, AThi, ATlo, Bhi, Blo, ATC, BC,
-           ssem, rsem, cssem, crsem, xssem, xrsem):
+def kernel(psi, pot, proj, ext, fin, out, T, R, RX, CS, CR, VB, AF, AThi, ATlo, Bhi, Blo, ATC, BC,
+           PB, A1, A2, B1, B2, A3, A4, B3, B4, ZR,
+           ssem, rsem, cssem, crsem, xssem, xrsem, pssem, prsem, gssem, grsem, zssem, zrsem, fssem, frsem,
+           wssem, wrsem):
     g = lax.axis_index("band")
     d = lax.axis_index("dom")
     ylo, z = g // 8, lax.rem(g, 8)
+    xi, yhi, c = d // 4, lax.rem(d // 2, 2), lax.rem(d, 2)
+    y = yhi * 2 + ylo
     dprev, dnext = lax.rem(d + ND - 1, ND), lax.rem(d + 1, ND)
 
     def peer(o):
@@ -51,8 +55,17 @@
     barrier = pltpu.get_barrier_semaphore()
     for o in range(NB - 1):
         pl.semaphore_signal(barrier, inc=1, device_id={"band": peer(o)}, device_id_type=MESH)
-    pl.semaphore_signal(barrier, inc=1, device_id={"dom": dprev}, device_id_type=MESH)
-    pl.semaphore_signal(barrier, inc=1, device_id={"dom": dnext}, device_id_type=MESH)
+    for k in range(1, ND):
+        pl.semaphore_signal(barrier, inc=1, device_id={"dom": lax.rem(d + k, ND)}, device_id_type=MESH)
+
+    def at_y(q):
+        return {"band": lax.rem(q, 2) * 8 + z, "dom": xi * 4 + (q // 2) * 2 + c}
+
+    def at_x(q):
+        return {"dom": q * 4 + yhi * 2 + c}
+
+    pl.semaphore_signal(barrier, inc=1, device_id={"band": (1 - ylo) * 8 + z, "dom": xi * 4 + (1 - yhi) * 2 + c},
+                        device_id_type=MESH)
 
     for r in range(RPZ):
         xy = (r // 8) * 16 + r % 8
@@ -61,7 +74,7 @@
         T[pl.ds(r, 128, stride=RPZ), :] = jnp.concatenate([a, b], axis=0).T
     T[pl.ds(128 * RPZ, RPZ), :] = T[pl.ds(0, RPZ), :]
 
-    pl.semaphore_wait(barrier, NB + 1)
+    pl.semaphore_wait(barrier, 31)
 
     def main_copy(o):
         p = peer(o)
@@ -99,8 +112,8 @@
         phi, plo = split(p)
         qhi, qlo = split(q)
         acc = acc + dot_nt(qhi, phi) + dot_nt(qhi, plo) + dot_nt(qlo, phi)
-    c = jnp.concatenate([acc, jnp.zeros((56, 64), F32)], axis=0)
-    chi, clo = split(c)
+    craw = jnp.concatenate([acc, jnp.zeros((56, 64), F32)], axis=0)
+    chi, clo = split(craw)
     ehi, elo = split(ext[...])
     msg = dot(ehi, chi) + dot(ehi, clo) + dot(elo, chi)
     msg = jnp.concatenate([msg, msg], axis=1)
@@ -184,8 +197,8 @@
 
     lax.fori_loop(0, 8, assemble, 0)
 
-    def product(t, _):
-        i, j = t // 8, lax.rem(t, 8)
+    def product(first, t):
+        i, j = t // 4, first + lax.rem(t, 4)
         rows = pl.ds(pl.multiple_of(i * 256, 256), 256)
         cols = pl.ds(pl.multiple_of(j * 256, 256), 256)
         a = AThi[rows, :]
@@ -194,24 +207,226 @@
         res = res * VOLUME
         out[2 * j, rows, :] = res[:, :128]
         out[2 * j + 1, rows, :] = res[:, 128:]
-        return 0
-
-    lax.fori_loop(0, 32, product, 0)
-
-    def symmetrize(t, _):
-        i, j = t // 8, lax.rem(t, 8)
-        ri = pl.ds(pl.multiple_of(i * 128, 128), 128)
-        rj = pl.ds(pl.multiple_of(j * 128, 128), 128)
-
-        @pl.when(i <= j)
-        def _():
-            s = 0.5 * (out[j, ri, :] + out[i, rj, :].T)
-            out[j, ri, :] = s
-            out[i, rj, :] = s.T
-        return 0
-
-    lax.fori_loop(0, 64, symmetrize, 0)
-
+
+    def matrix(first):
+        def body(t, _):
+            product(first, t)
+            return 0
+        lax.fori_loop(0, 16, body, 0)
+
+    def symmetrize():
+        def body(t, _):
+            i, j = t // 8, lax.rem(t, 8)
+            ri = pl.ds(pl.multiple_of(i * 128, 128), 128)
+            rj = pl.ds(pl.multiple_of(j * 128, 128), 128)
+
+            @pl.when(i <= j)
+            def _():
+                s = 0.5 * (out[j, ri, :] + out[i, rj, :].T)
+                out[j, ri, :] = s
+                out[i, rj, :] = s.T
+            return 0
+        lax.fori_loop(0, 64, body, 0)
+
+    other = d + 1 - 2 * c
+
+    def pair_copy(t):
+        return pltpu.make_async_remote_copy(
+            src_ref=out.at[(1 - c) * 8 + t], dst_ref=PB.at[t], send_sem=pssem.at[t], recv_sem=prsem.at[t],
+            device_id={"dom": other}, device_id_type=MESH)
+
+    matrix((1 - c) * 4)
+
+    @pl.when(c == 1)
+    def _():
+        symmetrize()
+
+    for t in range(8):
+        pair_copy(t).start()
+    matrix(c * 4)
+
+    @pl.when(c == 0)
+    def _():
+        symmetrize()
+
+    base = c * 8
+    for t in range(8):
+        pair_copy(t).wait_recv()
+
+    def add_pair(tile, ly, part):
+        rows = pl.ds(pl.multiple_of(ly * 512 + part * 256, 256), 256)
+        out[base + tile, rows, :] = out[base + tile, rows, :] + PB[tile, rows, :]
+
+    def rows_of(ly, at, count):
+        return pl.ds(pl.multiple_of(ly * 512 + at, 64), count)
+
+    def remote(src, dst, n, where):
+        return pltpu.make_async_remote_copy(
+            src_ref=src, dst_ref=dst, send_sem=gssem.at[n], recv_sem=grsem.at[n],
+            device_id=where, device_id_type=MESH)
+
+    class Ring:
+        def __init__(self, me, at, pieces, first, second, number):
+            self.me, self.pieces, self.first, self.second = me, pieces, first, second
+            self.plus, self.minus = at(lax.rem(me + 1, 4)), at(lax.rem(me + 3, 4))
+            self.number = number
+
+        def views(self, q, h):
+            return [out.at[v] for v in self.pieces(q, h)]
+
+        def copies(self, k):
+            me = self.me
+            q, h, buf, way = (
+                (me + 2, 0, self.first.at[0], self.plus),
+                (me + 2, 1, self.first.at[1], self.minus),
+                (me + 1, 1, self.second.at[0, 1], self.plus),
+                (me + 3, 0, self.second.at[1, 0], self.minus),
+                (me + 1, 0, self.second.at[0, 0], self.plus),
+                (me + 3, 1, self.second.at[1, 1], self.minus),
+            )[k]
+            views = self.views(lax.rem(q, 4), h)
+            return [remote(v, buf.at[i], self.number + 2 * k + i, way) for i, v in enumerate(views)]
+
+        def start(self, k):
+            for c_ in self.copies(k):
+                c_.start()
+
+        def wait_recv(self, k):
+            for c_ in self.copies(k):
+                c_.wait_recv()
+
+        def wait_send(self, k):
+            for c_ in self.copies(k):
+                c_.wait_send()
+
+        def add(self, q, h, *bufs):
+            for i, v in enumerate(self.pieces(lax.rem(q, 4), h)):
+                total = out[v]
+                for b in bufs:
+                    total = total + b[i]
+                out[v] = total
+
+        def relay(self):
+            self.wait_recv(0)
+            self.add(self.me + 1, 0, self.first.at[0])
+            self.start(4)
+            self.wait_recv(1)
+            self.add(self.me + 3, 1, self.first.at[1])
+            self.start(5)
+
+        def finish(self):
+            self.wait_recv(2)
+            self.wait_recv(3)
+            self.wait_recv(4)
+            self.wait_recv(5)
+            for h in range(2):
+                self.add(self.me, h, self.second.at[0, h], self.second.at[1, h])
+
+    def pieces_ax(q, h):
+        return [(base + h * 4 + q, pl.ds(ly * 512, 256), slice(None)) for ly in range(2)]
+
+    def pieces_by(q, h):
+        return [(base + (q // 2) * 4 + 2 * h + i, rows_of(lax.rem(q, 2), 256, 256), slice(None)) for i in range(2)]
+
+    def pieces_ay(q, h):
+        return [(base + (q // 2) * 4 + xi, rows_of(lax.rem(q, 2), h * 128, 128), slice(None))]
+
+    def pieces_bx(q, h):
+        return [(base + yhi * 4 + q, rows_of(ylo, 256 + h * 128, 128), slice(None))]
+
+    ax = Ring(xi, at_x, pieces_ax, A1, A2, 0)
+    by = Ring(y, at_y, pieces_by, B1, B2, 12)
+    ay = Ring(y, at_y, pieces_ay, A3, A4, 24)
+    bx = Ring(xi, at_x, pieces_bx, B3, B4, 36)
+
+    def add_ax(q, h):
+        for ly in range(2):
+            add_pair(h * 4 + lax.rem(q, 4), ly, 0)
+
+    def add_by(q, h):
+        q = lax.rem(q, 4)
+        for i in range(2):
+            add_pair((q // 2) * 4 + 2 * h + i, lax.rem(q, 2), 1)
+
+    order = ((2, 0, 0), (2, 1, 1), (1, 1, 2), (3, 0, 3))
+    for step, h, k in order:
+        add_ax(xi + step, h)
+        ax.start(k)
+        add_by(y + step, h)
+        by.start(k)
+    for step, h in ((1, 0), (3, 1)):
+        add_ax(xi + step, h)
+        add_by(y + step, h)
+    ax.relay()
+    by.relay()
+    for h in range(2):
+        add_ax(xi, h)
+        add_by(y, h)
+    ax.finish()
+    for k in range(4):
+        ay.start(k)
+    by.finish()
+    for k in range(4):
+        bx.start(k)
+    ay.relay()
+    bx.relay()
+    ay.finish()
+    bx.finish()
+
+    tile = yhi * 4 + xi
+
+    def z_copy(k):
+        q = lax.rem(z + k, 8)
+        return pltpu.make_async_remote_copy(
+            src_ref=out.at[base + tile, rows_of(ylo, q * 64, 64)], dst_ref=ZR.at[k - 1],
+            send_sem=zssem.at[k - 1], recv_sem=zrsem.at[k - 1],
+            device_id={"band": ylo * 8 + q}, device_id_type=MESH)
+
+    for k in (4, 3, 5, 2, 6, 1, 7):
+        z_copy(k).start()
+    total = out[base + tile, rows_of(ylo, z * 64, 64), :]
+    for k in range(1, 8):
+        z_copy(k).wait_recv()
+        total = total + ZR[k - 1]
+    at = pl.ds(pl.multiple_of(tile * 128, 128), 128)
+    fin[c, :, at] = total
+
+    def column(x_, h_):
+        return pl.ds(pl.multiple_of((h_ * 4 + x_) * 128, 128), 128)
+
+    def gather_copy(k):
+        px, ph = lax.rem(xi + k // 2, 4), lax.rem(yhi + k, 2)
+        return pltpu.make_async_remote_copy(
+            src_ref=fin.at[c, :, at], dst_ref=fin.at[c, :, at],
+            send_sem=fssem.at[k - 1], recv_sem=frsem.at[k - 1],
+            device_id={"dom": px * 4 + ph * 2 + c}, device_id_type=MESH)
+
+    def swap_copy(k):
+        px, ph = lax.rem(xi - k // 2 + 4, 4), lax.rem(yhi + k, 2)
+        part = fin.at[c, :, column(px, ph)]
+        return pltpu.make_async_remote_copy(
+            src_ref=part, dst_ref=part, send_sem=wssem.at[k], recv_sem=wrsem.at[k],
+            device_id={"dom": other}, device_id_type=MESH)
+
+    for k in range(1, 8):
+        gather_copy(k).start()
+    swap_copy(0).start()
+    for k in range(1, 8):
+        gather_copy(k).wait_recv()
+        swap_copy(k).start()
+    for k in range(8):
+        swap_copy(k).wait_recv()
+
+    for t in range(8):
+        pair_copy(t).wait_send()
+    for ring in (ax, by, ay, bx):
+        for k in range(6):
+            ring.wait_send(k)
+    for k in range(1, 8):
+        z_copy(k).wait_send()
+        gather_copy(k).wait_send()
+    for k in range(8):
+        swap_copy(k).wait_send()
     for o in range(NB - 1):
         main_copy(o).wait_send()
         coef_copy(o).wait_send()
@@ -240,10 +455,11 @@
     vm = pl.BlockSpec(memory_space=pltpu.VMEM)
     part = pl.pallas_call(
         kernel,
-        out_shape=jax.ShapeDtypeStruct((16, 1024, 128), F32),
+        out_shape=jax.ShapeDtypeStruct((2, 64, 1024), F32),
         in_specs=[vm] * 4,
         out_specs=vm,
         scratch_shapes=[
+            pltpu.VMEM((16, 1024, 128), F32),
             pltpu.VMEM((129 * RPZ, 128), F32),
             pltpu.VMEM((NB, CHUNK, 128), F32),
             pltpu.VMEM((NB, CH, 8, 128), F32),
@@ -257,20 +473,37 @@
             pltpu.VMEM((512, 2048), BF16),
             pltpu.VMEM((1024, 128), BF16),
             pltpu.VMEM((128, 2048), BF16),
+            pltpu.VMEM((8, 1024, 128), F32),
+            pltpu.VMEM((2, 2, 256, 128), F32),
+            pltpu.VMEM((2, 2, 2, 256, 128), F32),
+            pltpu.VMEM((2, 2, 256, 128), F32),
+            pltpu.VMEM((2, 2, 2, 256, 128), F32),
+            pltpu.VMEM((2, 1, 128, 128), F32),
+            pltpu.VMEM((2, 2, 1, 128, 128), F32),
+            pltpu.VMEM((2, 1, 128, 128), F32),
+            pltpu.VMEM((2, 2, 1, 128, 128), F32),
+            pltpu.VMEM((7, 64, 128), F32),
             pltpu.SemaphoreType.DMA((NB,)),
             pltpu.SemaphoreType.DMA((NB,)),
             pltpu.SemaphoreType.DMA((NB,)),
             pltpu.SemaphoreType.DMA((NB,)),
             pltpu.SemaphoreType.DMA((NB,)),
             pltpu.SemaphoreType.DMA((NB,)),
+            pltpu.SemaphoreType.DMA((8,)),
+            pltpu.SemaphoreType.DMA((8,)),
+            pltpu.SemaphoreType.DMA((48,)),
+            pltpu.SemaphoreType.DMA((48,)),
+            pltpu.SemaphoreType.DMA((7,)),
+            pltpu.SemaphoreType.DMA((7,)),
+            pltpu.SemaphoreType.DMA((7,)),
+            pltpu.SemaphoreType.DMA((7,)),
+            pltpu.SemaphoreType.DMA((8,)),
+            pltpu.SemaphoreType.DMA((8,)),
         ],
         compiler_params=pltpu.CompilerParams(
             collective_id=0, has_side_effects=True, vmem_limit_bytes=60 * 1024 * 1024),
     )(psi, pot, proj, ext)
-    rows = lax.psum_scatter(part, "band", scatter_dimension=1, tiled=True)
-    total = lax.psum(rows, "dom")
-    total = jnp.swapaxes(total.reshape(2, 8, 64, 128), 1, 2).reshape(2, 64, 1024)
-    return total[0], total[1]
+    return part[0], part[1]
 
 
 def solution(mesh):

time: 363 us -> 150 us (0.41)
  waiting for transfers between devices: 244 us -> 0 us
  Pallas kernels: 98.6 us -> 143 us
  between operations: 14.1 us -> 0.71 us
    psum x1 -> x0, waiting for transfers between devices: 145 us -> none  [on_device(): total = lax.psum(rows, 'dom')]
    reduce_scatter x1 -> x0, waiting for transfers between devices: 98.4 us -> none  [on_device(): rows = lax.psum_scatter(part, 'band', scatter_dimension=1, tiled=True)]
    pallas_call x1, Pallas kernels: 98.6 us -> 143 us  [on_device(): pl.pallas_call(kernel, out_shape=jax.ShapeDtypeStruct((2, 64, 1024), F32)...]
  transfers between devices with their start and end apart: 2 -> 0, of which waited for: 2 -> 0; matrix products, arithmetic and copies ran while one was open for 0% -> 0% of each run, Pallas kernels for 0% -> 0%
where the time goes in v2:
time: 150 us
  Pallas kernels  143 us (95%)
  local copies, waits for them, and re-layouts  3.31 us (2%)
  other arithmetic  3.18 us (2%)
    pallas_call x1, Pallas kernels, on_device(): pl.pallas_call(kernel, out_shape=jax.ShapeDtypeStruct((2, 64, 1024), F32)...  143 us

profile of v2, /device:TPU:1, one launch (start us, length us, event | category | flops | bytes accessed | tf_op | source)
XLA Modules:
  0.0 149.9 jit_solution(2670344113716233586)
XLA Ops:
  0.6 0.7 fusion.3
  1.4 0.7 fusion.4
  2.1 0.1 copy.12
  2.2 0.8 pad_maximum_fusion
  3.0 0.1 copy.11
  3.1 0.9 fusion.1
  4.0 0.1 mul.50
  4.1 0.1 mul.51
  4.3 0.1 mul.48
  4.3 0.2 mul.49
  4.7 0.7 pad.9.clone
  5.3 142.7 %shard_map.77 = f32[2,64,1024]{2,1,0:T(8,128)} custom-call(f32[4096,128]{1,0:T(8,128)} %bitcast.19, f32[64,128]{1,0:T(8,128)} %bitcast.27, f32[4608,128]{1,0:T(8,128)} %bitcast.18, f32[256,128]{1,0:T(8,128)} %bitcast.21), custom_call_target="tpu_custom_call" | custom-call | tf_op jit(solution)/shard_map/pallas_call | solution.py:456
  148.0 1.9 %slice_bitcast_fusion = (f32[64,1024]{1,0:T(8,128)}, f32[64,1024]{1,0:T(8,128)}) fusion(f32[2,64,1024]{2,1,0:T(8,128)} %shard_map.77), kind=kLoop, calls=%fused_computation | loop fusion | bytes 1048576 | tf_op jit(solution)/shard_map/squeeze | solution.py:506
  (8 shorter events, 0.1 us)

commit v3 on v1

v3 whole, which is shorter than its diff:
```python
import jax
import jax.numpy as jnp
from jax import lax
from jax.experimental import pallas as pl
from jax.experimental.pallas import tpu as pltpu
from jax.sharding import PartitionSpec as P

MESH = pl.DeviceIdType.MESH
F32 = jnp.float32
BF16 = jnp.bfloat16
NB = 16
ND = 16
CH = 8
RPZ = 32
CHUNK = (CH + 1) * RPZ
VOLUME = 1.0 / 131072.0
DZ = (0, 1, 7, 2, 6, 3, 5, 4)
OFFSETS = [(1, 0)] + [(dy, (8 - DZ[p]) % 8) for p in range(1, 8) for dy in (0, 1)]
STAGES = ((0, 5), (5, 7), (7, 8))
START = (0, 25, 49, 64)
HALF = (12, 12, 7)


def block_of(row, col):
    top = max(row, col)
    if top < 5:
        return col * 5 + row
    if top < 7:
        return 25 + col * 2 + row - 5 if col < 5 else 35 + (col - 5) * 7 + row
    return 49 + col if col < 7 else 56 + row


def split(x):
    hi = x.astype(BF16)
    return hi, (x - hi.astype(F32)).astype(BF16)


def dot(a, b):
    return lax.dot_general(a, b, (((1,), (0,)), ((), ())), preferred_element_type=F32)


def dot_exact(a, b):
    return lax.dot_general(a, b, (((1,), (0,)), ((), ())), precision=lax.Precision.HIGHEST,
                           preferred_element_type=F32)


def dot_nt(a, b):
    return lax.dot_general(a, b, (((1,), (1,)), ((), ())), preferred_element_type=F32)


def kernel(psi_in, pot, proj_in, hcor, dels, count, ham, corr,
           psi, proj, SP, M, T, R, RX, CS, CR, VB, AF, AThi, ATlo, Bhi, Blo, ATC, BC, PB,
           F1, F2, G1, G2, ZS, ZR, fin,
           lsem, ssem, rsem, cssem, crsem, xssem, xrsem, pssem, prsem, gssem, grsem,
           zssem, zrsem, fssem, frsem, wssem, wrsem):
    g = lax.axis_index("band")
    d = lax.axis_index("dom")
    ylo, z = g // 8, lax.rem(g, 8)
    xi, yhi, c = d // 4, lax.rem(d // 2, 2), lax.rem(d, 2)
    y = yhi * 2 + ylo
    dprev = lax.rem(d + ND - 1, ND)
    other = d + 1 - 2 * c

    def peer(o):
        dy, dz = OFFSETS[o]
        return lax.rem(ylo + dy, 2) * 8 + lax.rem(z + dz, 8)

    def source(o):
        dy, dz = OFFSETS[o]
        return lax.rem(ylo + dy, 2) * 8 + lax.rem(z - dz + 8, 8)

    def at_y(q):
        return {"band": lax.rem(q, 2) * 8 + z, "dom": xi * 4 + (q // 2) * 2 + c}

    def at_x(q):
        return {"dom": q * 4 + yhi * 2 + c}

    load_psi = pltpu.make_async_copy(psi_in, psi, lsem.at[0])
    load_proj = pltpu.make_async_copy(proj_in, proj, lsem.at[1])
    load_psi.start()
    load_proj.start()

    barrier = pltpu.get_barrier_semaphore()
    for o in range(NB - 1):
        pl.semaphore_signal(barrier, inc=1, device_id={"band": peer(o)}, device_id_type=MESH)
    for k in range(1, ND):
        pl.semaphore_signal(barrier, inc=1, device_id={"dom": lax.rem(d + k, ND)}, device_id_type=MESH)
    pl.semaphore_signal(barrier, inc=1, device_id={"band": (1 - ylo) * 8 + z, "dom": xi * 4 + (1 - yhi) * 2 + c},
                        device_id_type=MESH)

    load_psi.wait()
    for r in range(RPZ):
        xy = (r // 8) * 16 + r % 8
        a = psi[pl.ds(xy, 64, stride=64), :]
        b = psi[pl.ds(xy + 8, 64, stride=64), :]
        T[pl.ds(r, 128, stride=RPZ), :] = jnp.concatenate([a, b], axis=0).T
    T[pl.ds(128 * RPZ, RPZ), :] = T[pl.ds(0, RPZ), :]

    pl.semaphore_wait(barrier, 31)

    def main_copy(o):
        p = peer(o)
        return pltpu.make_async_remote_copy(
            src_ref=T.at[pl.ds(pl.multiple_of(p * (CH * RPZ), CH * RPZ), CHUNK)],
            dst_ref=R.at[g],
            send_sem=ssem.at[o], recv_sem=rsem.at[o],
            device_id={"band": p}, device_id_type=MESH)

    def coef_copy(o):
        p = peer(o)
        return pltpu.make_async_remote_copy(
            src_ref=CS.at[p], dst_ref=CR.at[g],
            send_sem=cssem.at[o], recv_sem=crsem.at[o],
            device_id={"band": p}, device_id_type=MESH)

    def x_copy(o):
        s = source(o) if o < NB - 1 else g
        return pltpu.make_async_remote_copy(
            src_ref=R.at[s].reshape(CH + 1, RPZ, 128).at[pl.ds(0, CH), pl.ds(0, 8)],
            dst_ref=RX.at[s],
            send_sem=xssem.at[o], recv_sem=xrsem.at[o],
            device_id={"dom": dprev}, device_id_type=MESH)

    for o in range(NB - 1):
        main_copy(o).start()

    R[g] = T[pl.ds(pl.multiple_of(g * (CH * RPZ), CH * RPZ), CHUNK), :]

    load_proj.wait()
    def project(t, acc):
        for x in range(4):
            xy = x * 16 + t
            p = jnp.concatenate([psi[pl.ds(xy, 64, stride=64), :], psi[pl.ds(xy + 8, 64, stride=64), :]], axis=1)
            q = jnp.concatenate([proj[pl.ds(xy, 72, stride=64), :], proj[pl.ds(xy + 8, 72, stride=64), :]], axis=1)
            phi, plo = split(p)
            qhi, qlo = split(q)
            acc = acc + dot_nt(qhi, phi) + dot_nt(qhi, plo) + dot_nt(qlo, phi)
        return acc

    acc = lax.fori_loop(0, 8, project, jnp.zeros((72, 64), F32))
    craw = jnp.concatenate([acc, jnp.zeros((56, 64), F32)], axis=0)
    x_copy(NB - 1).start()

    line = lax.broadcasted_iota(jnp.int32, (256, 128), 0)
    slot = lax.broadcasted_iota(jnp.int32, (256, 128), 1)
    spot = (line >> 4) * 5 + (line & 15)
    ext = jnp.where((line & 15) < 5, jnp.where(slot == spot, 1.0, 0.0), 0.0)
    srow = lax.broadcasted_iota(jnp.int32, (128, 128), 0)
    scol = lax.broadcasted_iota(jnp.int32, (128, 128), 1)
    SP[...] = jnp.zeros_like(SP)
    for t, ref in ((1, hcor), (2, dels)):
        inside = jnp.where((line & 15) >= 5 * t, jnp.where((line & 15) < 5 * t + 5, 1.0, 0.0), 0.0)

        def couple(a, ext):
            SP[0:18, 0:18] = ref[a]
            s = SP[...]
            s = (0.5 / VOLUME) * (s + s.T)
            used_col = jnp.clip(count[a] - slot, 0, 1).astype(F32)
            used_row = jnp.clip(count[a] - srow, 0, 1).astype(F32)
            left = jnp.where(spot - 5 * t == a * 18 + slot, used_col, 0.0) * inside
            right = jnp.where(scol == a * 18 + srow, used_row, 0.0)
            return ext + dot_exact(dot_exact(left, s), right)

        ext = lax.fori_loop(0, 4, couple, ext)
    chi, clo = split(craw)
    ehi, elo = split(ext)
    msg = dot(ehi, chi) + dot(ehi, clo) + dot(elo, chi)
    msg = jnp.concatenate([msg, msg], axis=1)
    CS[...] = msg.reshape(NB, 16, 128)
    CR[g] = CS[g]
    for o in range(NB - 1):
        coef_copy(o).start()

    v = 3.0 + pltpu.roll(pot[...], lax.rem(128 - g * CH, 128), 1)
    for zi in range(CH):
        wide = jnp.broadcast_to(v[:, zi:zi + 1], (64, 128))
        for half in range(2):
            for x in range(4):
                VB[zi, half, x * 8:(x + 1) * 8, :] = wide[x * 16 + half * 8:x * 16 + half * 8 + 8]

    low = lax.broadcasted_iota(jnp.int32, (RPZ, 128), 1) < 64
    low8 = lax.broadcasted_iota(jnp.int32, (8, 128), 1) < 64
    low16 = lax.broadcasted_iota(jnp.int32, (16, 128), 1) < 64
    last = lax.broadcasted_iota(jnp.int32, (8, 128), 0) == 7
    keep = lax.broadcasted_iota(jnp.int32, (16, 128), 0) < 5

    def merge(a, b, mask):
        return jnp.where(mask, a, pltpu.roll(b, 64, 1)), jnp.where(mask, pltpu.roll(a, 64, 1), b)

    def assemble(m, _):
        odd = lax.rem(m, 2)
        dz = odd * ((m + 1) // 2) + (1 - odd) * (8 - m // 2)
        s0 = lax.rem(z + dz, 8)
        s1 = s0 + 8
        rowsm = pl.ds(pl.multiple_of(m * 128, 128), 128)
        cols = pl.ds(pl.multiple_of(m * 256, 256), 128)
        cols2 = pl.ds(pl.multiple_of(m * 256 + 128, 128), 128)

        def column(zi):
            rows = pl.ds(zi * RPZ, RPZ)
            return merge(R[s0, rows, :], R[s1, rows, :], low)

        now = column(0)
        for zi in range(CH):
            nxt = column(zi + 1)
            halo = merge(RX[s0, zi], RX[s1, zi], low8)
            turned = []
            for half in range(2):
                turned.append([pltpu.roll(now[half][x * 8:(x + 1) * 8], 7, 0) for x in range(4)])
            for half in range(2):
                a = now[half]
                ax = jnp.concatenate([a[8:], halo[half]], axis=0)
                ay = jnp.concatenate(
                    [jnp.where(last, turned[1 - half][x], turned[half][x]) for x in range(4)], axis=0)
                h = VB[zi, half] * a - ax - ay - nxt[half]
                rows = pl.ds(half * 256 + zi * RPZ, RPZ)
                AF[rows, :] = a
                hi, lo = split(h)
                Bhi[rows, cols] = hi
                Blo[rows, cols] = lo
                hi, lo = split(a)
                Bhi[rows, cols2] = hi
                Blo[rows, cols2] = lo
            now = nxt
        hi, lo = split(AF[...].T)
        AThi[rowsm, :] = hi
        ATlo[rowsm, :] = lo
        cc, _ = merge(CR[s0], CR[s1], low16)
        chi, clo = split(cc)
        chi, clo = chi.astype(F32), clo.astype(F32)
        zero = jnp.zeros((16, 128), F32)
        pad = jnp.zeros((80, 128), F32)
        ahi = jnp.where(keep, chi, zero)
        alo = jnp.where(keep, clo, zero)
        ATC[rowsm, :] = jnp.concatenate([ahi, ahi, alo, pad], axis=0).T.astype(BF16)
        for t, at in ((1, cols), (2, cols2)):
            bhi = jnp.where(keep, pltpu.roll(chi, 16 - 5 * t, 0), zero)
            blo = jnp.where(keep, pltpu.roll(clo, 16 - 5 * t, 0), zero)
            BC[:, at] = jnp.concatenate([bhi, blo, bhi, pad], axis=0).astype(BF16)
        return 0

    def product(first, n, col, at):
        rows = pl.ds(pl.multiple_of(first * 128, 128), n * 128)
        cols = pl.ds(pl.multiple_of(col * 256, 256), 256)
        a = AThi[rows, :]
        res = dot(a, Bhi[:, cols]) + dot(a, Blo[:, cols]) + dot(ATlo[rows, :], Bhi[:, cols]) \
            + dot(ATC[rows, :], BC[:, cols])
        res = res * VOLUME
        for r in range(n):
            for mat in range(2):
                M[mat * 64 + at + r] = res[r * 128:(r + 1) * 128, mat * 128:(mat + 1) * 128].reshape(2, 4, 2, 8, 128)

    def loop(count_, body):
        def step(t, _):
            body(t)
            return 0
        lax.fori_loop(0, count_, step, 0)

    def even(k, l):
        s = 0.5 * (M[k].reshape(128, 128) + M[l].reshape(128, 128).T)
        M[k] = s.reshape(2, 4, 2, 8, 128)
        M[l] = s.T.reshape(2, 4, 2, 8, 128)

    def products(stage):
        if stage == 0:
            loop(5, lambda t: product(0, 2, t, t * 5))
            loop(5, lambda t: product(2, 2, t, t * 5 + 2))
            loop(5, lambda t: product(4, 1, t, t * 5 + 4))

            def pair(t):
                i, j = t // 5, lax.rem(t, 5)

                @pl.when(i <= j)
                def _():
                    even(j * 5 + i, i * 5 + j)
            loop(25, pair)
        elif stage == 1:
            loop(5, lambda t: product(5, 2, t, 25 + t * 2))
            for i in range(3):
                loop(2, lambda t: product(2 * i, 2, 5 + t, 35 + t * 7 + 2 * i))
            loop(2, lambda t: product(6, 1, 5 + t, 35 + t * 7 + 6))
            loop(10, lambda t: even(35 + (t // 5) * 7 + lax.rem(t, 5), 25 + lax.rem(t, 5) * 2 + t // 5))
            for i, j in ((5, 5), (5, 6), (6, 6)):
                even(block_of(i, j), block_of(j, i))
        else:
            loop(7, lambda t: product(7, 1, t, 49 + t))
            loop(4, lambda t: product(2 * t, 2, 7, 56 + 2 * t))
            loop(7, lambda t: even(56 + t, 49 + t))
            even(63, 63)

    def pair_copy(stage):
        k0, n = START[stage], START[stage + 1] - START[stage]
        return pltpu.make_async_remote_copy(
            src_ref=M.at[pl.ds((1 - c) * 64 + k0, n)], dst_ref=PB.at[pl.ds(k0, n)],
            send_sem=pssem.at[stage], recv_sem=prsem.at[stage],
            device_id={"dom": other}, device_id_type=MESH)

    base = c * 64

    def add_pair(stage):
        pair_copy(stage).wait_recv()

        def body(t):
            M[base + START[stage] + t] = M[base + START[stage] + t] + PB[START[stage] + t]
        loop(START[stage + 1] - START[stage], body)

    class Ring:
        def __init__(self, me, at, piece, first, second, number):
            self.me, self.piece, self.first, self.second = me, piece, first, second
            self.plus, self.minus = at(lax.rem(me + 1, 4)), at(lax.rem(me + 3, 4))
            self.number = number

        def copy(self, k):
            me = self.me
            q, h, buf, way = (
                (me + 2, 0, self.first(0), self.plus),
                (me + 2, 1, self.first(1), self.minus),
                (me + 1, 1, self.second(0, 1), self.plus),
                (me + 3, 0, self.second(1, 0), self.minus),
                (me + 1, 0, self.second(0, 0), self.plus),
                (me + 3, 1, self.second(1, 1), self.minus),
            )[k]
            return pltpu.make_async_remote_copy(
                src_ref=M.at[self.piece(lax.rem(q, 4), h)], dst_ref=buf,
                send_sem=gssem.at[self.number + k], recv_sem=grsem.at[self.number + k],
                device_id=way, device_id_type=MESH)

        def start(self):
            for k in range(4):
                self.copy(k).start()

        def add(self, q, h, *bufs):
            at = self.piece(lax.rem(q, 4), h)
            total = M[at]
            for b in bufs:
                total = total + b[...]
            M[at] = total

        def relay(self):
            self.copy(0).wait_recv()
            self.add(self.me + 1, 0, self.first(0))
            self.copy(4).start()
            self.copy(1).wait_recv()
            self.add(self.me + 3, 1, self.first(1))
            self.copy(5).start()

        def finish(self):
            for k in range(2, 6):
                self.copy(k).wait_recv()
            for h in range(2):
                self.add(self.me, h, self.second(0, h), self.second(1, h))

        def wait_send(self):
            for k in range(6):
                self.copy(k).wait_send()

    rings = []
    full = slice(None)
    for stage in range(3):
        k0, n = START[stage], START[stage + 1] - START[stage]
        na = HALF[stage]
        nb = n - na
        kb = k0 + na
        ha = (na // 2, na - na // 2)
        hb = (nb // 2, nb - nb // 2)

        def ax_piece(q, h, k0=k0, na=na):
            return (pl.ds(base + k0, na), h, q)

        def by_piece(q, h, kb=kb, nb=nb):
            return (pl.ds(base + kb, nb), lax.rem(q, 2), pl.ds(2 * h, 2), q // 2)

        def ay_piece(q, h, k0=k0, ha=ha):
            return (pl.ds(base + k0 + h * ha[0], ha[h]), lax.rem(q, 2), xi, q // 2)

        def bx_piece(q, h, kb=kb, hb=hb):
            return (pl.ds(base + kb + h * hb[0], hb[h]), ylo, q, yhi)

        def wide_first(k, n):
            return lambda h: F1.at[h, pl.ds(k, n)]

        def wide_second(k, n):
            return lambda w, h: F2.at[w, h, pl.ds(k, n)]

        def thin_first(k, hs):
            return lambda h: G1.at[pl.ds(k + h * hs[0], hs[h])]

        def thin_second(k, hs):
            return lambda w, h: G2.at[w, pl.ds(k + h * hs[0], hs[h])]

        rings.append((
            Ring(xi, at_x, ax_piece, wide_first(k0, na), wide_second(k0, na), stage * 24),
            Ring(y, at_y, by_piece, wide_first(kb, nb), wide_second(kb, nb), stage * 24 + 6),
            Ring(y, at_y, ay_piece, thin_first(k0, ha), thin_second(k0, ha), stage * 24 + 12),
            Ring(xi, at_x, bx_piece, thin_first(kb, hb), thin_second(kb, hb), stage * 24 + 18),
        ))

    def arrive(positions):
        for p in positions:
            for o in ((0,) if p == 0 else (2 * p - 1, 2 * p)):
                main_copy(o).wait_recv()
                x_copy(o).start()

    def ready(positions):
        for p in positions:
            for o in ((0, NB - 1) if p == 0 else (2 * p - 1, 2 * p)):
                x_copy(o).wait_recv()
                if o < NB - 1:
                    coef_copy(o).wait_recv()

    def build(stage):
        first, last_ = STAGES[stage]
        lax.fori_loop(first, last_, assemble, 0)
        products(stage)
        pair_copy(stage).start()

    def wide_start(stage):
        add_pair(stage)
        rings[stage][0].start()
        rings[stage][1].start()

    def wide_relay(stage):
        rings[stage][0].relay()
        rings[stage][1].relay()

    def wide_finish(stage):
        rings[stage][0].finish()
        rings[stage][2].start()
        rings[stage][1].finish()
        rings[stage][3].start()

    def thin_relay(stage):
        rings[stage][2].relay()
        rings[stage][3].relay()

    def thin_finish(stage):
        rings[stage][2].finish()
        rings[stage][3].finish()

    arrive(range(0, 5))
    ready(range(0, 5))
    build(0)
    wide_start(0)
    wide_relay(0)
    arrive(range(5, 7))
    wide_finish(0)
    ready(range(5, 7))
    build(1)
    thin_relay(0)
    wide_start(1)
    thin_finish(0)
    wide_relay(1)
    arrive(range(7, 8))
    wide_finish(1)
    ready(range(7, 8))
    build(2)
    thin_relay(1)
    wide_start(2)
    thin_finish(1)
    wide_relay(2)
    wide_finish(2)
    thin_relay(2)
    thin_finish(2)

    for i in range(8):
        for j in range(8):
            ZS[i, lax.rem(z + DZ[j], 8)] = M[base + block_of(i, j), ylo, xi, yhi]

    def z_copy(i):
        return pltpu.make_async_remote_copy(
            src_ref=ZS.at[i], dst_ref=ZR.at[i - 1],
            send_sem=zssem.at[i - 1], recv_sem=zrsem.at[i - 1],
            device_id={"band": ylo * 8 + lax.rem(z + DZ[i], 8)}, device_id_type=MESH)

    for i in range(7, 0, -1):
        z_copy(i).start()
    total = ZS[0]
    for i in range(1, 8):
        z_copy(i).wait_recv()
        total = total + ZR[i - 1]
    rows = pl.ds(pl.multiple_of(xi * 16 + yhi * 8, 8), 8)
    for j in range(4):
        lo, hi = merge(total[2 * j], total[2 * j + 1], low8)
        fin[c, rows, j * 128:(j + 1) * 128] = lo
        fin[c, rows, 512 + j * 128:512 + (j + 1) * 128] = hi

    def gather_copy(k):
        px, ph = lax.rem(xi + k // 2, 4), lax.rem(yhi + k, 2)
        return pltpu.make_async_remote_copy(
            src_ref=fin.at[c, rows], dst_ref=fin.at[c, rows],
            send_sem=fssem.at[k - 1], recv_sem=frsem.at[k - 1],
            device_id={"dom": px * 4 + ph * 2 + c}, device_id_type=MESH)

    def swap_copy(k):
        px, ph = lax.rem(xi - k // 2 + 4, 4), lax.rem(yhi + k, 2)
        part = fin.at[c, pl.ds(pl.multiple_of(px * 16 + ph * 8, 8), 8)]
        return pltpu.make_async_remote_copy(
            src_ref=part, dst_ref=part, send_sem=wssem.at[k], recv_sem=wrsem.at[k],
            device_id={"dom": other}, device_id_type=MESH)

    for k in (5, 4, 7, 6, 3, 2, 1):
        gather_copy(k).start()
    swap_copy(0).start()
    for k in range(1, 8):
        gather_copy(k).wait_recv()
        swap_copy(k).start()
    for k in range(8):
        swap_copy(k).wait_recv()
    ham[...] = fin[0]
    corr[...] = fin[1]

    for stage in range(3):
        pair_copy(stage).wait_send()
        for ring in rings[stage]:
            ring.wait_send()
    for k in range(1, 8):
        z_copy(k).wait_send()
        gather_copy(k).wait_send()
    for k in range(8):
        swap_copy(k).wait_send()
    for o in range(NB - 1):
        main_copy(o).wait_send()
        coef_copy(o).wait_send()
    for o in range(NB):
        x_copy(o).wait_send()


def on_device(wavefunctions, potential, projectors, hamiltonian_correction, delta_s, projector_count):
    vm = pl.BlockSpec(memory_space=pltpu.VMEM)
    hbm = pl.BlockSpec(memory_space=pl.ANY)
    dma = pltpu.SemaphoreType.DMA
    return pl.pallas_call(
        kernel,
        out_shape=(jax.ShapeDtypeStruct((64, 1024), F32), jax.ShapeDtypeStruct((64, 1024), F32)),
        in_specs=[hbm, vm, hbm, vm, vm, pl.BlockSpec(memory_space=pltpu.SMEM)],
        out_specs=(vm, vm),
        scratch_shapes=[
            pltpu.VMEM((4096, 128), F32),
            pltpu.VMEM((4608, 128), F32),
            pltpu.VMEM((128, 128), F32),
            pltpu.VMEM((128, 2, 4, 2, 8, 128), F32),
            pltpu.VMEM((129 * RPZ, 128), F32),
            pltpu.VMEM((NB, CHUNK, 128), F32),
            pltpu.VMEM((NB, CH, 8, 128), F32),
            pltpu.VMEM((NB, 16, 128), F32),
            pltpu.VMEM((NB, 16, 128), F32),
            pltpu.VMEM((CH, 2, RPZ, 128), F32),
            pltpu.VMEM((512, 128), F32),
            pltpu.VMEM((1024, 512), BF16),
            pltpu.VMEM((1024, 512), BF16),
            pltpu.VMEM((512, 2048), BF16),
            pltpu.VMEM((512, 2048), BF16),
            pltpu.VMEM((1024, 128), BF16),
            pltpu.VMEM((128, 2048), BF16),
            pltpu.VMEM((64, 2, 4, 2, 8, 128), F32),
            pltpu.VMEM((2, 64, 2, 8, 128), F32),
            pltpu.VMEM((2, 2, 64, 2, 8, 128), F32),
            pltpu.VMEM((64, 8, 128), F32),
            pltpu.VMEM((2, 64, 8, 128), F32),
            pltpu.VMEM((8, 8, 8, 128), F32),
            pltpu.VMEM((7, 8, 8, 128), F32),
            pltpu.VMEM((2, 64, 1024), F32),
            dma((2,)),
            dma((NB,)), dma((NB,)), dma((NB,)), dma((NB,)), dma((NB,)), dma((NB,)),
            dma((3,)), dma((3,)), dma((72,)), dma((72,)),
            dma((7,)), dma((7,)), dma((7,)), dma((7,)), dma((8,)), dma((8,)),
        ],
        compiler_params=pltpu.CompilerParams(
            collective_id=0, has_side_effects=True, vmem_limit_bytes=60 * 1024 * 1024),
    )(wavefunctions.reshape(4096, 128), potential.reshape(64, 128), projectors.reshape(72 * 64, 128),
      hamiltonian_correction, delta_s, projector_count)


def solution(mesh):
    placed = (
        P("band", "dom", None, None),
        P("dom", None, None),
        P("dom", None, None, None, None),
        P("dom", None, None),
        P("dom", None, None),
        P("dom"),
    )
    return jax.shard_map(
        on_device, mesh=mesh, in_specs=placed,
        out_specs=(P("band", None), P("band", None)), check_vma=False)
```

time: 363 us -> 160 us (0.44)
  waiting for transfers between devices: 244 us -> 0 us
  Pallas kernels: 98.6 us -> 153 us
  between operations: 14.1 us -> 0.64 us
    psum x1 -> x0, waiting for transfers between devices: 145 us -> none  [on_device(): total = lax.psum(rows, 'dom')]
    reduce_scatter x1 -> x0, waiting for transfers between devices: 98.4 us -> none  [on_device(): rows = lax.psum_scatter(part, 'band', scatter_dimension=1, tiled=True)]
    pallas_call x1, Pallas kernels: 98.6 us -> 153 us  [on_device(): pl.pallas_call(kernel, out_shape=(jax.ShapeDtypeStruct((64, 1024), F32),...]
    unnamed x1 -> x4, local copies, waits for them, and re-layouts: 0.05 us -> 6.13 us
  transfers between devices with their start and end apart: 2 -> 0, of which waited for: 2 -> 0; matrix products, arithmetic and copies ran while one was open for 0% -> 0% of each run, Pallas kernels for 0% -> 0%
where the time goes in v3:
time: 160 us
  Pallas kernels  153 us (96%)
  local copies, waits for them, and re-layouts  6.13 us (4%)
    pallas_call x1, Pallas kernels, on_device(): pl.pallas_call(kernel, out_shape=(jax.ShapeDtypeStruct((64, 1024), F32),...  153 us
    unnamed x4, local copies, waits for them, and re-layouts  6.13 us

profile of v3, /device:TPU:1, one launch (start us, length us, event | category | flops | bytes accessed | tf_op | source)
XLA Modules:
  0.0 159.5 jit_solution(607376536960991924)
XLA Ops:
  0.6 1.4 copy.8.hcor
  2.0 1.4 copy.9.dels
  3.4 152.8 %shard_map.77 = (f32[64,1024]{1,0:T(8,128)}, f32[64,1024]{1,0:T(8,128)}) custom-call(f32[4096,128]{1,0:T(8,128)} %bitcast.4, f32[64,128]{1,0:T(8,128)} %bitcast.5, f32[4608,128]{1,0:T(8,128)} %bitcast.3, f32[4,18,18]{2,1,0:T(8,128)} %copy.8.hcor, f32[4,18,18]{2,1,0:T(8,128)} %copy.9.dels, s32[4]{0:T(128)} %count.1), custom_call_target="tpu_custom_call" | custom-call | tf_op jit(solution)/shard_map/pallas_call | solution.py:532
  156.2 1.7 %copy.12 = f32[64,1024]{1,0:T(8,128)} copy(f32[64,1024]{1,0:T(8,128)} %get-tuple-element.4) | data formatting | bytes 524288
  157.9 1.7 %copy.13 = f32[64,1024]{1,0:T(8,128)} copy(f32[64,1024]{1,0:T(8,128)} %get-tuple-element.5) | data formatting | bytes 524288

commit v4 on v3

--- a/solution.py
+++ b/solution.py
@@ -121,7 +121,7 @@
             send_sem=xssem.at[o], recv_sem=xrsem.at[o],
             device_id={"dom": dprev}, device_id_type=MESH)
 
-    for o in range(NB - 1):
+    for o in range(9):
         main_copy(o).start()
 
     R[g] = T[pl.ds(pl.multiple_of(g * (CH * RPZ), CH * RPZ), CHUNK), :]
@@ -151,9 +151,11 @@
     for t, ref in ((1, hcor), (2, dels)):
         inside = jnp.where((line & 15) >= 5 * t, jnp.where((line & 15) < 5 * t + 5, 1.0, 0.0), 0.0)
 
+        for a in range(4):
+            SP[t - 1, a, 0:18, 0:18] = ref[:, a, :]
+
         def couple(a, ext):
-            SP[0:18, 0:18] = ref[a]
-            s = SP[...]
+            s = SP[t - 1, a]
             s = (0.5 / VOLUME) * (s + s.T)
             used_col = jnp.clip(count[a] - slot, 0, 1).astype(F32)
             used_row = jnp.clip(count[a] - srow, 0, 1).astype(F32)
@@ -437,12 +439,18 @@
         rings[stage][2].finish()
         rings[stage][3].finish()
 
-    arrive(range(0, 5))
+    arrive(range(0, 4))
+    for o in range(9, 13):
+        main_copy(o).start()
+    arrive(range(4, 5))
     ready(range(0, 5))
     build(0)
     wide_start(0)
     wide_relay(0)
-    arrive(range(5, 7))
+    arrive(range(5, 6))
+    for o in range(13, 15):
+        main_copy(o).start()
+    arrive(range(6, 7))
     wide_finish(0)
     ready(range(5, 7))
     build(1)
@@ -537,7 +545,7 @@
         scratch_shapes=[
             pltpu.VMEM((4096, 128), F32),
             pltpu.VMEM((4608, 128), F32),
-            pltpu.VMEM((128, 128), F32),
+            pltpu.VMEM((2, 4, 128, 128), F32),
             pltpu.VMEM((128, 2, 4, 2, 8, 128), F32),
             pltpu.VMEM((129 * RPZ, 128), F32),
             pltpu.VMEM((NB, CHUNK, 128), F32),
@@ -568,7 +576,7 @@
         compiler_params=pltpu.CompilerParams(
             collective_id=0, has_side_effects=True, vmem_limit_bytes=60 * 1024 * 1024),
     )(wavefunctions.reshape(4096, 128), potential.reshape(64, 128), projectors.reshape(72 * 64, 128),
-      hamiltonian_correction, delta_s, projector_count)
+      jnp.swapaxes(hamiltonian_correction, 0, 1), jnp.swapaxes(delta_s, 0, 1), projector_count)
 
 
 def solution(mesh):

time: 160 us -> 135 us (0.84)
  Pallas kernels: 153 us -> 131 us
  local copies, waits for them, and re-layouts: 6.13 us -> 3.34 us
    pallas_call x1, Pallas kernels: 153 us -> 131 us  [on_device(): pl.pallas_call(kernel, out_shape=(jax.ShapeDtypeStruct((64, 1024), F32),...]
    unnamed x4 -> x2, local copies, waits for them, and re-layouts: 6.13 us -> 3.34 us
where the time goes in v4:
time: 135 us
  Pallas kernels  131 us (97%)
  local copies, waits for them, and re-layouts  3.34 us (2%)
    pallas_call x1, Pallas kernels, on_device(): pl.pallas_call(kernel, out_shape=(jax.ShapeDtypeStruct((64, 1024), F32),...  131 us
    unnamed x2, local copies, waits for them, and re-layouts  3.34 us

profile of v4, /device:TPU:1, one launch (start us, length us, event | category | flops | bytes accessed | tf_op | source)
XLA Modules:
  0.0 134.5 jit_solution(16598508422242377338)
XLA Ops:
  0.6 130.6 %shard_map.77 = (f32[64,1024]{1,0:T(8,128)}, f32[64,1024]{1,0:T(8,128)}) custom-call(f32[4096,128]{1,0:T(8,128)} %bitcast.6, f32[64,128]{1,0:T(8,128)} %bitcast.9, f32[4608,128]{1,0:T(8,128)} %bitcast.5, f32[18,4,18]{2,1,0:T(4,128)} %bitcast.7, f32[18,4,18]{2,1,0:T(4,128)} %bitcast.8, s32[4]{0:T(128)} %count.1), custom_call_target="tpu_custom_call" | custom-call | tf_op jit(solution)/shard_map/pallas_call | solution.py:540
  131.2 1.7 %copy.10 = f32[64,1024]{1,0:T(8,128)} copy(f32[64,1024]{1,0:T(8,128)} %get-tuple-element.4) | data formatting | bytes 524288
  132.9 1.7 %copy.11 = f32[64,1024]{1,0:T(8,128)} copy(f32[64,1024]{1,0:T(8,128)} %get-tuple-element.5) | data formatting | bytes 524288

commit v5 on v4

--- a/solution.py
+++ b/solution.py
@@ -48,9 +48,9 @@
     return lax.dot_general(a, b, (((1,), (1,)), ((), ())), preferred_element_type=F32)
 
 
-def kernel(psi_in, pot, proj_in, hcor, dels, count, ham, corr,
+def kernel(psi_in, pot, proj_in, hcor, dels, count, fin,
            psi, proj, SP, M, T, R, RX, CS, CR, VB, AF, AThi, ATlo, Bhi, Blo, ATC, BC, PB,
-           F1, F2, G1, G2, ZS, ZR, fin,
+           F1, F2, FX, FY, G2, ZS, ZR, TOT,
            lsem, ssem, rsem, cssem, crsem, xssem, xrsem, pssem, prsem, gssem, grsem,
            zssem, zrsem, fssem, frsem, wssem, wrsem):
     g = lax.axis_index("band")
@@ -356,6 +356,33 @@
             for k in range(6):
                 self.copy(k).wait_send()
 
+    class Direct:
+        def __init__(self, me, at, piece, buf, number):
+            self.me, self.at, self.piece, self.buf, self.number = me, at, piece, buf, number
+
+        def copy(self, k):
+            q = lax.rem(self.me + k, 4)
+            return pltpu.make_async_remote_copy(
+                src_ref=M.at[self.piece(q)], dst_ref=self.buf(k - 1),
+                send_sem=gssem.at[self.number + k - 1], recv_sem=grsem.at[self.number + k - 1],
+                device_id=self.at(q), device_id_type=MESH)
+
+        def start(self):
+            for k in (2, 1, 3):
+                self.copy(k).start()
+
+        def finish(self):
+            at = self.piece(self.me)
+            total = M[at]
+            for k in (1, 3, 2):
+                self.copy(k).wait_recv()
+                total = total + self.buf(k - 1)[...]
+            M[at] = total
+
+        def wait_send(self):
+            for k in range(1, 4):
+                self.copy(k).wait_send()
+
     rings = []
     full = slice(None)
     for stage in range(3):
@@ -363,8 +390,6 @@
         na = HALF[stage]
         nb = n - na
         kb = k0 + na
-        ha = (na // 2, na - na // 2)
-        hb = (nb // 2, nb - nb // 2)
 
         def ax_piece(q, h, k0=k0, na=na):
             return (pl.ds(base + k0, na), h, q)
@@ -372,11 +397,17 @@
         def by_piece(q, h, kb=kb, nb=nb):
             return (pl.ds(base + kb, nb), lax.rem(q, 2), pl.ds(2 * h, 2), q // 2)
 
-        def ay_piece(q, h, k0=k0, ha=ha):
-            return (pl.ds(base + k0 + h * ha[0], ha[h]), lax.rem(q, 2), xi, q // 2)
-
-        def bx_piece(q, h, kb=kb, hb=hb):
-            return (pl.ds(base + kb + h * hb[0], hb[h]), ylo, q, yhi)
+        def ax_whole(q, k0=k0, na=na):
+            return (pl.ds(base + k0, na), full, q)
+
+        def by_whole(q, kb=kb, nb=nb):
+            return (pl.ds(base + kb, nb), lax.rem(q, 2), full, q // 2)
+
+        def ay_piece(q, k0=k0, na=na):
+            return (pl.ds(base + k0, na), lax.rem(q, 2), xi, q // 2)
+
+        def bx_piece(q, kb=kb, nb=nb):
+            return (pl.ds(base + kb, nb), ylo, q, yhi)
 
         def wide_first(k, n):
             return lambda h: F1.at[h, pl.ds(k, n)]
@@ -384,24 +415,25 @@
         def wide_second(k, n):
             return lambda w, h: F2.at[w, h, pl.ds(k, n)]
 
-        def thin_first(k, hs):
-            return lambda h: G1.at[pl.ds(k + h * hs[0], hs[h])]
-
-        def thin_second(k, hs):
-            return lambda w, h: G2.at[w, pl.ds(k + h * hs[0], hs[h])]
-
-        rings.append((
-            Ring(xi, at_x, ax_piece, wide_first(k0, na), wide_second(k0, na), stage * 24),
-            Ring(y, at_y, by_piece, wide_first(kb, nb), wide_second(kb, nb), stage * 24 + 6),
-            Ring(y, at_y, ay_piece, thin_first(k0, ha), thin_second(k0, ha), stage * 24 + 12),
-            Ring(xi, at_x, bx_piece, thin_first(kb, hb), thin_second(kb, hb), stage * 24 + 18),
+        def thin(k, n):
+            return lambda i: G2.at[i, pl.ds(k, n)]
+
+        number = stage * 24
+        if stage < 2:
+            wide = (Ring(xi, at_x, ax_piece, wide_first(k0, na), wide_second(k0, na), number),
+                    Ring(y, at_y, by_piece, wide_first(kb, nb), wide_second(kb, nb), number + 6))
+        else:
+            wide = (Direct(xi, at_x, ax_whole, lambda i: FX.at[i], number),
+                    Direct(y, at_y, by_whole, lambda i: FY.at[i], number + 6))
+        rings.append(wide + (
+            Direct(y, at_y, ay_piece, thin(k0, na), number + 12),
+            Direct(xi, at_x, bx_piece, thin(kb, nb), number + 18),
         ))
 
-    def arrive(positions):
-        for p in positions:
-            for o in ((0,) if p == 0 else (2 * p - 1, 2 * p)):
-                main_copy(o).wait_recv()
-                x_copy(o).start()
+    def arrive(*offsets):
+        for o in offsets:
+            main_copy(o).wait_recv()
+            x_copy(o).start()
 
     def ready(positions):
         for p in positions:
@@ -431,64 +463,72 @@
         rings[stage][1].finish()
         rings[stage][3].start()
 
-    def thin_relay(stage):
-        rings[stage][2].relay()
-        rings[stage][3].relay()
-
     def thin_finish(stage):
         rings[stage][2].finish()
         rings[stage][3].finish()
-
-    arrive(range(0, 4))
+        z_send(stage)
+
+    Z_PARTS = (
+        [(i, 0, 5) for i in range(5)],
+        [(i, 5, 2) for i in range(5)] + [(5, 0, 7), (6, 0, 7)],
+        [(7, 0, 8)] + [(i, 7, 1) for i in range(6, -1, -1)],
+    )
+
+    def z_copy(stage, i, j, n):
+        return pltpu.make_async_remote_copy(
+            src_ref=ZS.at[i, pl.ds(j, n)], dst_ref=ZR.at[i - 1, pl.ds(j, n)],
+            send_sem=zssem.at[stage * 7 + i - 1], recv_sem=zrsem.at[stage * 7 + i - 1],
+            device_id={"band": ylo * 8 + lax.rem(z + DZ[i], 8)}, device_id_type=MESH)
+
+    def z_send(stage):
+        for i, j, n in Z_PARTS[stage]:
+            for t in range(j, j + n):
+                ZS[i, t] = M[base + block_of(i, t), ylo, xi, yhi]
+            if i > 0:
+                z_copy(stage, i, j, n).start()
+
+    def z_add(stage):
+        for i, j, n in sorted(Z_PARTS[stage]):
+            if i > 0:
+                z_copy(stage, i, j, n).wait_recv()
+                for t in range(j, j + n):
+                    at = lax.rem(z + 8 - DZ[i] + DZ[t], 8)
+                    TOT[at] = TOT[at] + ZR[i - 1, t]
+
+    arrive(0, 1, 2, 3, 4, 5, 7)
     for o in range(9, 13):
         main_copy(o).start()
-    arrive(range(4, 5))
+    arrive(6, 8)
     ready(range(0, 5))
     build(0)
     wide_start(0)
     wide_relay(0)
-    arrive(range(5, 6))
+    arrive(9, 11)
     for o in range(13, 15):
         main_copy(o).start()
-    arrive(range(6, 7))
+    arrive(10, 12)
     wide_finish(0)
     ready(range(5, 7))
     build(1)
-    thin_relay(0)
+    thin_finish(0)
     wide_start(1)
-    thin_finish(0)
     wide_relay(1)
-    arrive(range(7, 8))
-    wide_finish(1)
+    arrive(13, 14)
     ready(range(7, 8))
     build(2)
-    thin_relay(1)
+    wide_finish(1)
     wide_start(2)
     thin_finish(1)
-    wide_relay(2)
     wide_finish(2)
-    thin_relay(2)
     thin_finish(2)
-
-    for i in range(8):
-        for j in range(8):
-            ZS[i, lax.rem(z + DZ[j], 8)] = M[base + block_of(i, j), ylo, xi, yhi]
-
-    def z_copy(i):
-        return pltpu.make_async_remote_copy(
-            src_ref=ZS.at[i], dst_ref=ZR.at[i - 1],
-            send_sem=zssem.at[i - 1], recv_sem=zrsem.at[i - 1],
-            device_id={"band": ylo * 8 + lax.rem(z + DZ[i], 8)}, device_id_type=MESH)
-
-    for i in range(7, 0, -1):
-        z_copy(i).start()
-    total = ZS[0]
-    for i in range(1, 8):
-        z_copy(i).wait_recv()
-        total = total + ZR[i - 1]
+    for t in range(8):
+        TOT[lax.rem(z + DZ[t], 8)] = ZS[0, t]
+    for stage in range(3):
+        z_add(stage)
+
     rows = pl.ds(pl.multiple_of(xi * 16 + yhi * 8, 8), 8)
     for j in range(4):
-        lo, hi = merge(total[2 * j], total[2 * j + 1], low8)
+        lo, hi = merge(TOT[2 * j], TOT[2 * j + 1], low8)
         fin[c, rows, j * 128:(j + 1) * 128] = lo
         fin[c, rows, 512 + j * 128:512 + (j + 1) * 128] = hi
 
@@ -514,15 +554,15 @@
         swap_copy(k).start()
     for k in range(8):
         swap_copy(k).wait_recv()
-    ham[...] = fin[0]
-    corr[...] = fin[1]
 
     for stage in range(3):
         pair_copy(stage).wait_send()
         for ring in rings[stage]:
             ring.wait_send()
+        for i, j, n in Z_PARTS[stage]:
+            if i > 0:
+                z_copy(stage, i, j, n).wait_send()
     for k in range(1, 8):
-        z_copy(k).wait_send()
         gather_copy(k).wait_send()
     for k in range(8):
         swap_copy(k).wait_send()
@@ -537,11 +577,11 @@
     vm = pl.BlockSpec(memory_space=pltpu.VMEM)
     hbm = pl.BlockSpec(memory_space=pl.ANY)
     dma = pltpu.SemaphoreType.DMA
-    return pl.pallas_call(
+    both = pl.pallas_call(
         kernel,
-        out_shape=(jax.ShapeDtypeStruct((64, 1024), F32), jax.ShapeDtypeStruct((64, 1024), F32)),
+        out_shape=jax.ShapeDtypeStruct((2, 64, 1024), F32),
         in_specs=[hbm, vm, hbm, vm, vm, pl.BlockSpec(memory_space=pltpu.SMEM)],
-        out_specs=(vm, vm),
+        out_specs=vm,
         scratch_shapes=[
             pltpu.VMEM((4096, 128), F32),
             pltpu.VMEM((4608, 128), F32),
@@ -563,20 +603,22 @@
             pltpu.VMEM((64, 2, 4, 2, 8, 128), F32),
             pltpu.VMEM((2, 64, 2, 8, 128), F32),
             pltpu.VMEM((2, 2, 64, 2, 8, 128), F32),
-            pltpu.VMEM((64, 8, 128), F32),
-            pltpu.VMEM((2, 64, 8, 128), F32),
+            pltpu.VMEM((3, 7, 2, 2, 8, 128), F32),
+            pltpu.VMEM((3, 8, 4, 8, 128), F32),
+            pltpu.VMEM((3, 64, 8, 128), F32),
             pltpu.VMEM((8, 8, 8, 128), F32),
             pltpu.VMEM((7, 8, 8, 128), F32),
-            pltpu.VMEM((2, 64, 1024), F32),
+            pltpu.VMEM((8, 8, 128), F32),
             dma((2,)),
             dma((NB,)), dma((NB,)), dma((NB,)), dma((NB,)), dma((NB,)), dma((NB,)),
             dma((3,)), dma((3,)), dma((72,)), dma((72,)),
-            dma((7,)), dma((7,)), dma((7,)), dma((7,)), dma((8,)), dma((8,)),
+            dma((21,)), dma((21,)), dma((7,)), dma((7,)), dma((8,)), dma((8,)),
         ],
         compiler_params=pltpu.CompilerParams(
             collective_id=0, has_side_effects=True, vmem_limit_bytes=60 * 1024 * 1024),
     )(wavefunctions.reshape(4096, 128), potential.reshape(64, 128), projectors.reshape(72 * 64, 128),
       jnp.swapaxes(hamiltonian_correction, 0, 1), jnp.swapaxes(delta_s, 0, 1), projector_count)
+    return both[0], both[1]
 
 
 def solution(mesh):

time: 135 us -> 129 us (0.956)
  Pallas kernels: 131 us -> 126 us
  local copies, waits for them, and re-layouts: 3.34 us -> 1.87 us
    pallas_call x1, Pallas kernels: 131 us -> 126 us  [on_device(): pl.pallas_call(kernel, out_shape=jax.ShapeDtypeStruct((2, 64, 1024), F32)...]
    unnamed x2 -> x0, local copies, waits for them, and re-layouts: 3.34 us -> none
    squeeze x0 -> x1, local copies, waits for them, and re-layouts: none -> 1.87 us  [on_device(): return (both[0], both[1])]
where the time goes in v5:
time: 129 us
  Pallas kernels  126 us (98%)
  local copies, waits for them, and re-layouts  1.87 us (1%)
    pallas_call x1, Pallas kernels, on_device(): pl.pallas_call(kernel, out_shape=jax.ShapeDtypeStruct((2, 64, 1024), F32)...  126 us

profile of v5, /device:TPU:1, one launch (start us, length us, event | category | flops | bytes accessed | tf_op | source)
XLA Modules:
  0.0 128.8 jit_solution(17412318102355647868)
XLA Ops:
  0.6 126.3 %shard_map.77 = f32[2,64,1024]{2,1,0:T(8,128)} custom-call(f32[4096,128]{1,0:T(8,128)} %bitcast.10, f32[64,128]{1,0:T(8,128)} %bitcast.13, f32[4608,128]{1,0:T(8,128)} %bitcast.9, f32[18,4,18]{2,1,0:T(4,128)} %bitcast.11, f32[18,4,18]{2,1,0:T(4,128)} %bitcast.12, s32[4]{0:T(128)} %count.1), custom_call_target="tpu_custom_call" | custom-call | tf_op jit(solution)/shard_map/pallas_call | solution.py:580
  127.0 1.9 %slice_bitcast_fusion = (f32[64,1024]{1,0:T(8,128)}, f32[64,1024]{1,0:T(8,128)}) fusion(f32[2,64,1024]{2,1,0:T(8,128)} %shard_map.77), kind=kLoop, calls=%fused_computation | loop fusion | bytes 1048576 | tf_op jit(solution)/shard_map/squeeze | solution.py:621

commit v6 on v5

--- a/solution.py
+++ b/solution.py
@@ -189,22 +189,49 @@
     def merge(a, b, mask):
         return jnp.where(mask, a, pltpu.roll(b, 64, 1)), jnp.where(mask, pltpu.roll(a, 64, 1), b)
 
-    def assemble(m, _):
+    def place(m):
         odd = lax.rem(m, 2)
         dz = odd * ((m + 1) // 2) + (1 - odd) * (8 - m // 2)
         s0 = lax.rem(z + dz, 8)
-        s1 = s0 + 8
-        rowsm = pl.ds(pl.multiple_of(m * 128, 128), 128)
-        cols = pl.ds(pl.multiple_of(m * 256, 256), 128)
-        cols2 = pl.ds(pl.multiple_of(m * 256 + 128, 128), 128)
-
-        def column(zi):
-            rows = pl.ds(zi * RPZ, RPZ)
-            return merge(R[s0, rows, :], R[s1, rows, :], low)
-
-        now = column(0)
+        at = pl.multiple_of(m * 128, 128)
+        return s0, s0 + 8, pl.ds(at, 128), pl.ds(pl.multiple_of(1024 + m * 128, 128), 128)
+
+    def column(s0, s1, zi):
+        rows = pl.ds(zi * RPZ, RPZ)
+        return merge(R[s0, rows, :], R[s1, rows, :], low)
+
+    def assemble_psi(m, _):
+        s0, s1, cols, cols2 = place(m)
         for zi in range(CH):
-            nxt = column(zi + 1)
+            now = column(s0, s1, zi)
+            for half in range(2):
+                rows = pl.ds(half * 256 + zi * RPZ, RPZ)
+                AF[rows, :] = now[half]
+                hi, lo = split(now[half])
+                Bhi[rows, cols2] = hi
+                Blo[rows, cols2] = lo
+        hi, lo = split(AF[...].T)
+        AThi[cols, :] = hi
+        ATlo[cols, :] = lo
+        cc, _ = merge(CR[s0], CR[s1], low16)
+        chi, clo = split(cc)
+        chi, clo = chi.astype(F32), clo.astype(F32)
+        zero = jnp.zeros((16, 128), F32)
+        pad = jnp.zeros((80, 128), F32)
+        ahi = jnp.where(keep, chi, zero)
+        alo = jnp.where(keep, clo, zero)
+        ATC[cols, :] = jnp.concatenate([ahi, ahi, alo, pad], axis=0).T.astype(BF16)
+        for t, at in ((1, cols), (2, cols2)):
+            bhi = jnp.where(keep, pltpu.roll(chi, 16 - 5 * t, 0), zero)
+            blo = jnp.where(keep, pltpu.roll(clo, 16 - 5 * t, 0), zero)
+            BC[:, at] = jnp.concatenate([bhi, blo, bhi, pad], axis=0).astype(BF16)
+        return 0
+
+    def assemble_h(m, _):
+        s0, s1, cols, _ = place(m)
+        now = column(s0, s1, 0)
+        for zi in range(CH):
+            nxt = column(s0, s1, zi + 1)
             halo = merge(RX[s0, zi], RX[s1, zi], low8)
             turned = []
             for half in range(2):
@@ -216,41 +243,23 @@
                     [jnp.where(last, turned[1 - half][x], turned[half][x]) for x in range(4)], axis=0)
                 h = VB[zi, half] * a - ax - ay - nxt[half]
                 rows = pl.ds(half * 256 + zi * RPZ, RPZ)
-                AF[rows, :] = a
                 hi, lo = split(h)
                 Bhi[rows, cols] = hi
                 Blo[rows, cols] = lo
-                hi, lo = split(a)
-                Bhi[rows, cols2] = hi
-                Blo[rows, cols2] = lo
             now = nxt
-        hi, lo = split(AF[...].T)
-        AThi[rowsm, :] = hi
-        ATlo[rowsm, :] = lo
-        cc, _ = merge(CR[s0], CR[s1], low16)
-        chi, clo = split(cc)
-        chi, clo = chi.astype(F32), clo.astype(F32)
-        zero = jnp.zeros((16, 128), F32)
-        pad = jnp.zeros((80, 128), F32)
-        ahi = jnp.where(keep, chi, zero)
-        alo = jnp.where(keep, clo, zero)
-        ATC[rowsm, :] = jnp.concatenate([ahi, ahi, alo, pad], axis=0).T.astype(BF16)
-        for t, at in ((1, cols), (2, cols2)):
-            bhi = jnp.where(keep, pltpu.roll(chi, 16 - 5 * t, 0), zero)
-            blo = jnp.where(keep, pltpu.roll(clo, 16 - 5 * t, 0), zero)
-            BC[:, at] = jnp.concatenate([bhi, blo, bhi, pad], axis=0).astype(BF16)
         return 0
 
-    def product(first, n, col, at):
-        rows = pl.ds(pl.multiple_of(first * 128, 128), n * 128)
-        cols = pl.ds(pl.multiple_of(col * 256, 256), 256)
+    def product(mat, row, n, col, m, at, down, right):
+        rows = pl.ds(pl.multiple_of(row * 128, 128), n * 128)
+        cols = pl.ds(pl.multiple_of(mat * 1024 + col * 128, 128), m * 128)
         a = AThi[rows, :]
         res = dot(a, Bhi[:, cols]) + dot(a, Blo[:, cols]) + dot(ATlo[rows, :], Bhi[:, cols]) \
             + dot(ATC[rows, :], BC[:, cols])
         res = res * VOLUME
         for r in range(n):
-            for mat in range(2):
-                M[mat * 64 + at + r] = res[r * 128:(r + 1) * 128, mat * 128:(mat + 1) * 128].reshape(2, 4, 2, 8, 128)
+            for k in range(m):
+                M[mat * 64 + at + r * down + k * right] = \
+                    res[r * 128:(r + 1) * 128, k * 128:(k + 1) * 128].reshape(2, 4, 2, 8, 128)
 
     def loop(count_, body):
         def step(t, _):
@@ -263,12 +272,25 @@
         M[k] = s.reshape(2, 4, 2, 8, 128)
         M[l] = s.T.reshape(2, 4, 2, 8, 128)
 
-    def products(stage):
+    def products(stage, mat):
         if stage == 0:
-            loop(5, lambda t: product(0, 2, t, t * 5))
-            loop(5, lambda t: product(2, 2, t, t * 5 + 2))
-            loop(5, lambda t: product(4, 1, t, t * 5 + 4))
-
+            loop(4, lambda t: product(mat, (t // 2) * 2, 2, lax.rem(t, 2) * 2, 2,
+                                      lax.rem(t, 2) * 10 + (t // 2) * 2, 1, 5))
+            loop(2, lambda t: product(mat, 4, 1, 2 * t, 2, 10 * t + 4, 1, 5))
+            loop(2, lambda t: product(mat, 2 * t, 2, 4, 1, 20 + 2 * t, 1, 5))
+            product(mat, 4, 1, 4, 1, 24, 1, 5)
+        elif stage == 1:
+            loop(3, lambda t: product(mat, 2 * t, 2, 5, 2, 35 + 2 * t, 1, 7))
+            product(mat, 6, 1, 5, 2, 41, 1, 7)
+            loop(2, lambda t: product(mat, 5, 2, 2 * t, 2, 25 + 4 * t, 1, 2))
+            product(mat, 5, 2, 4, 1, 33, 1, 2)
+        else:
+            loop(4, lambda t: product(mat, 2 * t, 2, 7, 1, 56 + 2 * t, 1, 1))
+            loop(3, lambda t: product(mat, 7, 1, 2 * t, 2, 49 + 2 * t, 1, 1))
+            product(mat, 7, 1, 6, 1, 55, 1, 1)
+
+    def evens(stage):
+        if stage == 0:
             def pair(t):
                 i, j = t // 5, lax.rem(t, 5)
 
@@ -277,16 +299,10 @@
                     even(j * 5 + i, i * 5 + j)
             loop(25, pair)
         elif stage == 1:
-            loop(5, lambda t: product(5, 2, t, 25 + t * 2))
-            for i in range(3):
-                loop(2, lambda t: product(2 * i, 2, 5 + t, 35 + t * 7 + 2 * i))
-            loop(2, lambda t: product(6, 1, 5 + t, 35 + t * 7 + 6))
             loop(10, lambda t: even(35 + (t // 5) * 7 + lax.rem(t, 5), 25 + lax.rem(t, 5) * 2 + t // 5))
             for i, j in ((5, 5), (5, 6), (6, 6)):
                 even(block_of(i, j), block_of(j, i))
         else:
-            loop(7, lambda t: product(7, 1, t, 49 + t))
-            loop(4, lambda t: product(2 * t, 2, 7, 56 + 2 * t))
             loop(7, lambda t: even(56 + t, 49 + t))
             even(63, 63)
 
@@ -435,18 +451,28 @@
             main_copy(o).wait_recv()
             x_copy(o).start()
 
-    def ready(positions):
-        for p in positions:
-            for o in ((0, NB - 1) if p == 0 else (2 * p - 1, 2 * p)):
-                x_copy(o).wait_recv()
-                if o < NB - 1:
-                    coef_copy(o).wait_recv()
-
-    def build(stage):
+    def overlap_part(stage):
         first, last_ = STAGES[stage]
-        lax.fori_loop(first, last_, assemble, 0)
-        products(stage)
-        pair_copy(stage).start()
+        for o in ((0,) if stage == 0 else ()) + tuple(range(max(1, 2 * first - 1), 2 * last_ - 1)):
+            coef_copy(o).wait_recv()
+        lax.fori_loop(first, last_, assemble_psi, 0)
+        products(stage, 1)
+
+        @pl.when(c == 0)
+        def _():
+            pair_copy(stage).start()
+
+    def energy_part(stage):
+        first, last_ = STAGES[stage]
+        for o in ((NB - 1, 0) if stage == 0 else ()) + tuple(range(max(1, 2 * first - 1), 2 * last_ - 1)):
+            x_copy(o).wait_recv()
+        lax.fori_loop(first, last_, assemble_h, 0)
+        products(stage, 0)
+        evens(stage)
+
+        @pl.when(c == 1)
+        def _():
+            pair_copy(stage).start()
 
     def wide_start(stage):
         add_pair(stage)
@@ -499,23 +525,22 @@
     for o in range(9, 13):
         main_copy(o).start()
     arrive(6, 8)
-    ready(range(0, 5))
-    build(0)
+    overlap_part(0)
+    for o in range(13, 15):
+        main_copy(o).start()
+    energy_part(0)
     wide_start(0)
     wide_relay(0)
-    arrive(9, 11)
-    for o in range(13, 15):
-        main_copy(o).start()
-    arrive(10, 12)
+    arrive(9, 11, 10, 12)
+    overlap_part(1)
     wide_finish(0)
-    ready(range(5, 7))
-    build(1)
+    energy_part(1)
+    wide_start(1)
     thin_finish(0)
-    wide_start(1)
+    arrive(13, 14)
+    overlap_part(2)
     wide_relay(1)
-    arrive(13, 14)
-    ready(range(7, 8))
-    build(2)
+    energy_part(2)
     wide_finish(1)
     wide_start(2)
     thin_finish(1)

time: 129 us -> 127 us (0.984)
  Pallas kernels: 126 us -> 124 us
    pallas_call x1, Pallas kernels: 126 us -> 124 us  [on_device(): pl.pallas_call(kernel, out_shape=jax.ShapeDtypeStruct((2, 64, 1024), F32)...]
where the time goes in v6:
time: 127 us; the launch traced here: 126 us
  Pallas kernels  124 us (98%)
  local copies, waits for them, and re-layouts  1.87 us (1%)
    pallas_call x1, Pallas kernels, on_device(): pl.pallas_call(kernel, out_shape=jax.ShapeDtypeStruct((2, 64, 1024), F32)...  124 us

profile of v6, /device:TPU:1, one launch (start us, length us, event | category | flops | bytes accessed | tf_op | source)
XLA Modules:
  0.0 126.4 jit_solution(9216297769987981707)
XLA Ops:
  0.6 123.9 %shard_map.77 = f32[2,64,1024]{2,1,0:T(8,128)} custom-call(f32[4096,128]{1,0:T(8,128)} %bitcast.10, f32[64,128]{1,0:T(8,128)} %bitcast.13, f32[4608,128]{1,0:T(8,128)} %bitcast.9, f32[18,4,18]{2,1,0:T(4,128)} %bitcast.11, f32[18,4,18]{2,1,0:T(4,128)} %bitcast.12, s32[4]{0:T(128)} %count.1), custom_call_target="tpu_custom_call" | custom-call | tf_op jit(solution)/shard_map/pallas_call | solution.py:605
  124.5 1.9 %slice_bitcast_fusion = (f32[64,1024]{1,0:T(8,128)}, f32[64,1024]{1,0:T(8,128)}) fusion(f32[2,64,1024]{2,1,0:T(8,128)} %shard_map.77), kind=kLoop, calls=%fused_computation | loop fusion | bytes 1048576 | tf_op jit(solution)/shard_map/squeeze | solution.py:646

commit v7 on v6

--- a/solution.py
+++ b/solution.py
@@ -50,9 +50,9 @@
 
 def kernel(psi_in, pot, proj_in, hcor, dels, count, fin,
            psi, proj, SP, M, T, R, RX, CS, CR, VB, AF, AThi, ATlo, Bhi, Blo, ATC, BC, PB,
-           F1, F2, FX, FY, G2, ZS, ZR, TOT,
+           F1, F2, FX, FY, G2, ZS, ZR, TOT, HX,
            lsem, ssem, rsem, cssem, crsem, xssem, xrsem, pssem, prsem, gssem, grsem,
-           zssem, zrsem, fssem, frsem, wssem, wrsem):
+           zssem, zrsem, fssem, frsem, wssem, wrsem, hxsem, hsem):
     g = lax.axis_index("band")
     d = lax.axis_index("dom")
     ylo, z = g // 8, lax.rem(g, 8)
@@ -121,8 +121,32 @@
             send_sem=xssem.at[o], recv_sem=xrsem.at[o],
             device_id={"dom": dprev}, device_id_type=MESH)
 
+    home_copy = pltpu.make_async_remote_copy(
+        src_ref=T.reshape(129, RPZ, 128).at[pl.ds(0, 128), pl.ds(0, 8)], dst_ref=HX,
+        send_sem=hxsem.at[0], recv_sem=hxsem.at[1],
+        device_id={"dom": dprev}, device_id_type=MESH)
+
+    def halo_copy(o):
+        p = peer(o)
+        return pltpu.make_async_remote_copy(
+            src_ref=HX.at[pl.ds(pl.multiple_of(p * CH, CH), CH)], dst_ref=RX.at[g],
+            send_sem=hsem.at[o], recv_sem=xrsem.at[o],
+            device_id={"band": p}, device_id_type=MESH)
+
+    def send_far(*offsets):
+        for o in offsets:
+            main_copy(o).start()
+
+            @pl.when(c == 1)
+            def _():
+                halo_copy(o).start()
+
     for o in range(9):
         main_copy(o).start()
+
+    @pl.when(c == 0)
+    def _():
+        home_copy.start()
 
     R[g] = T[pl.ds(pl.multiple_of(g * (CH * RPZ), CH * RPZ), CHUNK), :]
 
@@ -449,7 +473,12 @@
     def arrive(*offsets):
         for o in offsets:
             main_copy(o).wait_recv()
-            x_copy(o).start()
+            if o < 9:
+                x_copy(o).start()
+            else:
+                @pl.when(c == 1)
+                def _():
+                    x_copy(o).start()
 
     def overlap_part(stage):
         first, last_ = STAGES[stage]
@@ -522,12 +551,15 @@
                     TOT[at] = TOT[at] + ZR[i - 1, t]
 
     arrive(0, 1, 2, 3, 4, 5, 7)
-    for o in range(9, 13):
-        main_copy(o).start()
+
+    @pl.when(c == 1)
+    def _():
+        home_copy.wait_recv()
+
+    send_far(9, 10, 11, 12)
     arrive(6, 8)
     overlap_part(0)
-    for o in range(13, 15):
-        main_copy(o).start()
+    send_far(13, 14)
     energy_part(0)
     wide_start(0)
     wide_relay(0)
@@ -594,8 +626,18 @@
     for o in range(NB - 1):
         main_copy(o).wait_send()
         coef_copy(o).wait_send()
-    for o in range(NB):
+    for o in (*range(9), NB - 1):
         x_copy(o).wait_send()
+
+    @pl.when(c == 0)
+    def _():
+        home_copy.wait_send()
+
+    @pl.when(c == 1)
+    def _():
+        for o in range(9, NB - 1):
+            x_copy(o).wait_send()
+            halo_copy(o).wait_send()
 
 
 def on_device(wavefunctions, potential, projectors, hamiltonian_correction, delta_s, projector_count):
@@ -634,10 +676,12 @@
             pltpu.VMEM((8, 8, 8, 128), F32),
             pltpu.VMEM((7, 8, 8, 128), F32),
             pltpu.VMEM((8, 8, 128), F32),
+            pltpu.VMEM((128, 8, 128), F32),
             dma((2,)),
             dma((NB,)), dma((NB,)), dma((NB,)), dma((NB,)), dma((NB,)), dma((NB,)),
             dma((3,)), dma((3,)), dma((72,)), dma((72,)),
             dma((21,)), dma((21,)), dma((7,)), dma((7,)), dma((8,)), dma((8,)),
+            dma((2,)), dma((NB,)),
         ],
         compiler_params=pltpu.CompilerParams(
             collective_id=0, has_side_effects=True, vmem_limit_bytes=60 * 1024 * 1024),

time: 127 us -> 128 us (level)
    pallas_call x1, Pallas kernels: 124 us -> 125 us  [on_device(): pl.pallas_call(kernel, out_shape=jax.ShapeDtypeStruct((2, 64, 1024), F32)...]
where the time goes in v7:
time: 128 us
  Pallas kernels  125 us (98%)
  local copies, waits for them, and re-layouts  1.87 us (1%)
    pallas_call x1, Pallas kernels, on_device(): pl.pallas_call(kernel, out_shape=jax.ShapeDtypeStruct((2, 64, 1024), F32)...  125 us

profile of v7, /device:TPU:1, one launch (start us, length us, event | category | flops | bytes accessed | tf_op | source)
XLA Modules:
  0.0 127.8 jit_solution(1081975575418572886)
XLA Ops:
  0.6 125.3 %shard_map.77 = f32[2,64,1024]{2,1,0:T(8,128)} custom-call(f32[4096,128]{1,0:T(8,128)} %bitcast.10, f32[64,128]{1,0:T(8,128)} %bitcast.13, f32[4608,128]{1,0:T(8,128)} %bitcast.9, f32[18,4,18]{2,1,0:T(4,128)} %bitcast.11, f32[18,4,18]{2,1,0:T(4,128)} %bitcast.12, s32[4]{0:T(128)} %count.1), custom_call_target="tpu_custom_call" | custom-call | tf_op jit(solution)/shard_map/pallas_call | solution.py:647
  126.0 1.9 %slice_bitcast_fusion = (f32[64,1024]{1,0:T(8,128)}, f32[64,1024]{1,0:T(8,128)}) fusion(f32[2,64,1024]{2,1,0:T(8,128)} %shard_map.77), kind=kLoop, calls=%fused_computation | loop fusion | bytes 1048576 | tf_op jit(solution)/shard_map/squeeze | solution.py:690

commit v8 on v7

--- a/solution.py
+++ b/solution.py
@@ -559,8 +559,8 @@
     send_far(9, 10, 11, 12)
     arrive(6, 8)
     overlap_part(0)
+    energy_part(0)
     send_far(13, 14)
-    energy_part(0)
     wide_start(0)
     wide_relay(0)
     arrive(9, 11, 10, 12)
@@ -569,11 +569,11 @@
     energy_part(1)
     wide_start(1)
     thin_finish(0)
+    wide_relay(1)
     arrive(13, 14)
     overlap_part(2)
-    wide_relay(1)
+    wide_finish(1)
     energy_part(2)
-    wide_finish(1)
     wide_start(2)
     thin_finish(1)
     wide_finish(2)

time: 128 us -> 129 us (level)
  no operation moved by 1% of the time
where the time goes in v8:
time: 129 us; the launch traced here: 128 us
  Pallas kernels  126 us (98%)
  local copies, waits for them, and re-layouts  1.87 us (1%)
    pallas_call x1, Pallas kernels, on_device(): pl.pallas_call(kernel, out_shape=jax.ShapeDtypeStruct((2, 64, 1024), F32)...  126 us

profile of v8, /device:TPU:1, one launch (start us, length us, event | category | flops | bytes accessed | tf_op | source)
XLA Modules:
  0.0 128.4 jit_solution(17819143218011759522)
XLA Ops:
  0.6 125.9 %shard_map.77 = f32[2,64,1024]{2,1,0:T(8,128)} custom-call(f32[4096,128]{1,0:T(8,128)} %bitcast.10, f32[64,128]{1,0:T(8,128)} %bitcast.13, f32[4608,128]{1,0:T(8,128)} %bitcast.9, f32[18,4,18]{2,1,0:T(4,128)} %bitcast.11, f32[18,4,18]{2,1,0:T(4,128)} %bitcast.12, s32[4]{0:T(128)} %count.1), custom_call_target="tpu_custom_call" | custom-call | tf_op jit(solution)/shard_map/pallas_call | solution.py:647
  126.5 1.9 %slice_bitcast_fusion = (f32[64,1024]{1,0:T(8,128)}, f32[64,1024]{1,0:T(8,128)}) fusion(f32[2,64,1024]{2,1,0:T(8,128)} %shard_map.77), kind=kLoop, calls=%fused_computation | loop fusion | bytes 1048576 | tf_op jit(solution)/shard_map/squeeze | solution.py:690

commit v9 on v6

--- a/solution.py
+++ b/solution.py
@@ -172,6 +172,8 @@
     CR[g] = CS[g]
     for o in range(NB - 1):
         coef_copy(o).start()
+    for o in (10, 12):
+        main_copy(o).start()
 
     v = 3.0 + pltpu.roll(pot[...], lax.rem(128 - g * CH, 128), 1)
     for zi in range(CH):
@@ -522,12 +524,11 @@
                     TOT[at] = TOT[at] + ZR[i - 1, t]
 
     arrive(0, 1, 2, 3, 4, 5, 7)
-    for o in range(9, 13):
+    for o in (9, 11, 14):
         main_copy(o).start()
     arrive(6, 8)
     overlap_part(0)
-    for o in range(13, 15):
-        main_copy(o).start()
+    main_copy(13).start()
     energy_part(0)
     wide_start(0)
     wide_relay(0)
@@ -535,9 +536,9 @@
     overlap_part(1)
     wide_finish(0)
     energy_part(1)
+    arrive(13, 14)
     wide_start(1)
     thin_finish(0)
-    arrive(13, 14)
     overlap_part(2)
     wide_relay(1)
     energy_part(2)

time: 127 us -> 128 us (level)
  no operation moved by 1% of the time
where the time goes in v9:
time: 128 us; the launch traced here: 127 us
  Pallas kernels  125 us (98%)
  local copies, waits for them, and re-layouts  1.87 us (1%)
    pallas_call x1, Pallas kernels, on_device(): pl.pallas_call(kernel, out_shape=jax.ShapeDtypeStruct((2, 64, 1024), F32)...  125 us

profile of v9, /device:TPU:1, one launch (start us, length us, event | category | flops | bytes accessed | tf_op | source)
XLA Modules:
  0.0 127.4 jit_solution(4988659992641852263)
XLA Ops:
  0.6 124.9 %shard_map.77 = f32[2,64,1024]{2,1,0:T(8,128)} custom-call(f32[4096,128]{1,0:T(8,128)} %bitcast.10, f32[64,128]{1,0:T(8,128)} %bitcast.13, f32[4608,128]{1,0:T(8,128)} %bitcast.9, f32[18,4,18]{2,1,0:T(4,128)} %bitcast.11, f32[18,4,18]{2,1,0:T(4,128)} %bitcast.12, s32[4]{0:T(128)} %count.1), custom_call_target="tpu_custom_call" | custom-call | tf_op jit(solution)/shard_map/pallas_call | solution.py:606
  125.5 1.9 %slice_bitcast_fusion = (f32[64,1024]{1,0:T(8,128)}, f32[64,1024]{1,0:T(8,128)}) fusion(f32[2,64,1024]{2,1,0:T(8,128)} %shard_map.77), kind=kLoop, calls=%fused_computation | loop fusion | bytes 1048576 | tf_op jit(solution)/shard_map/squeeze | solution.py:647

commit v10 on v9

--- a/solution.py
+++ b/solution.py
@@ -540,12 +540,12 @@
     wide_start(1)
     thin_finish(0)
     overlap_part(2)
+    energy_part(2)
+    wide_start(2)
     wide_relay(1)
-    energy_part(2)
     wide_finish(1)
-    wide_start(2)
+    wide_finish(2)
     thin_finish(1)
-    wide_finish(2)
     thin_finish(2)
     for t in range(8):
         TOT[lax.rem(z + DZ[t], 8)] = ZS[0, t]

time: 128 us -> 127 us (level)
  no operation moved by 1% of the time
where the time goes in v10:
time: 127 us
  Pallas kernels  124 us (98%)
  local copies, waits for them, and re-layouts  1.87 us (1%)
    pallas_call x1, Pallas kernels, on_device(): pl.pallas_call(kernel, out_shape=jax.ShapeDtypeStruct((2, 64, 1024), F32)...  124 us

profile of v10, /device:TPU:1, one launch (start us, length us, event | category | flops | bytes accessed | tf_op | source)
XLA Modules:
  0.0 126.7 jit_solution(18102253483289811368)
XLA Ops:
  0.6 124.2 %shard_map.77 = f32[2,64,1024]{2,1,0:T(8,128)} custom-call(f32[4096,128]{1,0:T(8,128)} %bitcast.10, f32[64,128]{1,0:T(8,128)} %bitcast.13, f32[4608,128]{1,0:T(8,128)} %bitcast.9, f32[18,4,18]{2,1,0:T(4,128)} %bitcast.11, f32[18,4,18]{2,1,0:T(4,128)} %bitcast.12, s32[4]{0:T(128)} %count.1), custom_call_target="tpu_custom_call" | custom-call | tf_op jit(solution)/shard_map/pallas_call | solution.py:606
  124.8 1.9 %slice_bitcast_fusion = (f32[64,1024]{1,0:T(8,128)}, f32[64,1024]{1,0:T(8,128)}) fusion(f32[2,64,1024]{2,1,0:T(8,128)} %shard_map.77), kind=kLoop, calls=%fused_computation | loop fusion | bytes 1048576 | tf_op jit(solution)/shard_map/squeeze | solution.py:647
